TPU v7x, 512 devices: a 4x2x32 block of a 4x8x32 slice. The times are simulated.
512 devices in a mesh: groups: 2 (over y), plane: 32 (over z), depth: 4 (over x), tok: 2 (over core).
Axes of the slice: x: 4, y: 2, z: 32, core: 2. Of those that a mesh axis runs over, the one named last changes fastest.
The devices are a block of a 4x8x32 slice.
Arguments:
- tokens: bfloat16 [4096, 2048], P(('groups', 'plane', 'depth', 'tok')), parts along dimension 0, may hold values from -6 to 6
- expert_ids: int32 [4096, 4], P(('groups', 'plane', 'depth', 'tok')), parts along dimension 0, may hold values from 0 to 31, as said below
- slot_index: int32 [4096, 4], P(('groups', 'plane', 'depth', 'tok')), parts along dimension 0, may hold values from 0 to 7, as said below
- route_weight: bfloat16 [4096, 4], P(('groups', 'plane', 'depth', 'tok')), parts along dimension 0, may hold values from 0.099609375 to 1
- shared_gate: bfloat16 [2048], replicated, may hold values from -0.125 to 0.125
- shared_gate_up: bfloat16 [2, 2048, 5632], P(None, None, 'plane'), may hold values from -0.125 to 0.125
- shared_down: bfloat16 [5632, 2048], P('plane'), may hold values from -0.078125 to 0.078125
- expert_gate_up: bfloat16 [32, 2, 2048, 1408], P('plane', None, None, ('depth', 'tok')), may hold values from -0.125 to 0.125
- expert_down: bfloat16 [32, 1408, 2048], P('plane', ('depth', 'tok')), may hold values from -0.15625 to 0.15625
Outputs:
- mixed: bfloat16 [4096, 2048], P(('groups', 'plane', 'depth', 'tok')), parts along dimension 0
There are 2 independent parts, one for each index of `groups`. A program takes and returns all parts, laid end to end along the dimension named above; an argument that names none is the same for every part. Nothing has to cross between parts.
Inputs may be any that keep to these rules, and one draw needn't show every extreme that they name: `expert_ids`: each row names 4 different experts. Among the choices of the rows of one device that name the same expert, slot_index takes each value from 0 to their count minus one exactly once, in an order that varies from draw to draw; the capacity 2 is filled on some devices.
All inputs are finite; a program needn't handle non-finite values.
Results may differ from a plain program's by a relative error of at most 0.019.
Values may be sent and summed in bfloat16 or wider, within the bound.
No kernel may reach another device: no remote copies, remote signals or barrier semaphores. Data moves between devices by JAX's collectives and lax.ppermute only.
A program may use at most 64 MiB of HBM per device.

v0:
```python
import jax
import jax.numpy as jnp
from jax import lax
from jax.experimental import pallas as pl
from jax.experimental.pallas import tpu as pltpu
from jax.sharding import PartitionSpec as P

LANES = 128
KERNEL_VMEM = 14 << 20


def from_offset(block, axis, offset):
    size, cores = lax.axis_size(axis), lax.axis_size("tok")
    pairs = [
        (((i + (-offset if t % 2 else offset)) % size) * cores + t, i * cores + t)
        for i in range(size)
        for t in range(cores)
    ]
    return lax.ppermute(block, (axis, "tok"), pairs)


def from_core(block):
    size = lax.axis_size("tok")
    return lax.ppermute(block, "tok", [((i + 1) % size, i) for i in range(size)])


def far_groups(planes, near):
    return [[r + near * f for f in range(planes // near)] for r in range(near)]


def gather_planes(block, near):
    groups = far_groups(lax.axis_size("plane"), near)
    own = lax.all_gather(block, "plane", axis_index_groups=groups)
    return jnp.stack([own] + [from_offset(own, "plane", k) for k in (1, 2, -1)])


def reduce_planes(blocks, near):
    sent = blocks.astype(jnp.bfloat16)
    total = blocks[0]
    for j, k in ((1, 1), (2, 2), (3, -1)):
        total = total + from_offset(sent[j], "plane", -k).astype(jnp.float32)
    arrived = lax.all_to_all(
        total.astype(jnp.bfloat16),
        "plane",
        split_axis=0,
        concat_axis=0,
        tiled=True,
        axis_index_groups=far_groups(lax.axis_size("plane"), near),
    )
    return arrived.astype(jnp.float32).sum(axis=0)


def from_chip(block, partner):
    size = lax.axis_size("depth")
    return lax.ppermute(block, "depth", [(partner(i, size), i) for i in range(size)])


def weight_partner(place, size):
    return place ^ 1


def row_partner(place, size):
    return size - 1 - place


def expert_kernel(own_ref, other_ref, *refs):
    shards = (len(refs) - 5) // 2
    gate_up_refs, down_refs = refs[:shards], refs[shards : 2 * shards]
    kept_ref, sent_ref, gate_up, down, sems = refs[2 * shards :]
    copies = []
    for s in range(shards):
        copies.append(pltpu.make_async_copy(gate_up_refs[s], gate_up.at[s], sems.at[2 * s]))
        copies.append(pltpu.make_async_copy(down_refs[s], down.at[s], sems.at[2 * s + 1]))
    for copy in copies:
        copy.start()
    rows = jnp.concatenate([own_ref[...], other_ref[...]])
    contract = (((1,), (1,)), ((), ()))
    total = None
    for s in range(shards):
        copies[2 * s].wait()
        gate = lax.dot_general(rows, gate_up[s, 0], contract, preferred_element_type=jnp.float32)
        up = lax.dot_general(rows, gate_up[s, 1], contract, preferred_element_type=jnp.float32)
        hidden = (gate / (1.0 + jnp.exp(-gate)) * up).astype(jnp.bfloat16)
        copies[2 * s + 1].wait()
        part = jnp.dot(hidden, down[s], preferred_element_type=jnp.float32)
        total = part if total is None else total + part
    half = own_ref.shape[0]
    kept_ref[...] = total[:half]
    sent_ref[...] = total[half:].astype(jnp.bfloat16)


def expert_partials(own, other, gate_ups, downs):
    rows, width = own.shape
    units = downs[0].shape[0]
    vmem, anywhere = pl.BlockSpec(memory_space=pltpu.VMEM), pl.BlockSpec(memory_space=pl.ANY)
    shards = len(downs)
    return pl.pallas_call(
        expert_kernel,
        out_shape=(
            jax.ShapeDtypeStruct((rows, width), jnp.float32),
            jax.ShapeDtypeStruct((rows, width), jnp.bfloat16),
        ),
        in_specs=[vmem, vmem] + [anywhere] * (2 * shards),
        out_specs=(vmem, vmem),
        scratch_shapes=[
            pltpu.VMEM((shards, 2, units, width), jnp.bfloat16),
            pltpu.VMEM((shards, units, width), jnp.bfloat16),
            pltpu.SemaphoreType.DMA((2 * shards,)),
        ],
        compiler_params=pltpu.CompilerParams(vmem_limit_bytes=KERNEL_VMEM),
        cost_estimate=pl.CostEstimate(
            flops=12 * shards * rows * width * units,
            bytes_accessed=6 * shards * units * width,
            transcendentals=2 * shards * rows * units,
        ),
    )(own, other, *gate_ups, *downs)


def gated_rows(token_rows, gate_up):
    gate_part = jnp.dot(token_rows, gate_up[0], preferred_element_type=jnp.float32)
    up_part = jnp.dot(token_rows, gate_up[1], preferred_element_type=jnp.float32)
    return lax.optimization_barrier((jax.nn.silu(gate_part) * up_part).astype(jnp.bfloat16))


def on_device(
    tokens,
    expert_ids,
    slot_index,
    route_weight,
    shared_gate,
    shared_gate_up,
    shared_down,
    expert_gate_up,
    expert_down,
):
    planes = lax.axis_size("plane")
    tok_rows, width = tokens.shape
    choices = expert_ids.shape[1]
    capacity = max(2, tok_rows * choices // planes)
    near = 4
    slots = planes * capacity

    code = jnp.where(slot_index < capacity, expert_ids * capacity + slot_index, -1)
    notes = jnp.concatenate([code.astype(jnp.bfloat16), route_weight], axis=1)
    notes = jnp.pad(notes, ((0, 0), (0, LANES - 2 * choices)))
    gathered = gather_planes(jnp.concatenate([tokens, notes], axis=1), near)
    gathered = gathered.reshape(planes * tok_rows, width + LANES)
    all_tokens = gathered[:, :width]
    codes = gathered[:, width : width + choices].astype(jnp.float32)
    weights = gathered[:, width + choices : width + 2 * choices].astype(jnp.float32)

    mine = (lax.axis_index("plane") * capacity).astype(jnp.float32)
    count = planes * tok_rows
    here = lax.broadcasted_iota(jnp.int32, (count, slots), 0) // tok_rows
    column = lax.broadcasted_iota(jnp.int32, (count, slots), 1)
    slot_code = mine + (column % capacity).astype(jnp.float32)
    hit = jnp.any(codes[:, None, :] == slot_code[:, :, None], axis=2)
    pick = (hit & (here == column // capacity)).astype(jnp.bfloat16)
    pick = lax.optimization_barrier(pick)
    matched = (codes >= mine) & (codes < mine + capacity)
    factor = jnp.sum(jnp.where(matched, weights, 0.0), axis=1, keepdims=True)

    rows = lax.dot_general(
        pick, all_tokens, (((0,), (0,)), ((), ())), preferred_element_type=jnp.float32
    ).astype(jnp.bfloat16)
    gate_up, down = expert_gate_up[0].swapaxes(1, 2), expert_down[0]
    gate_up_chip = from_chip(gate_up, weight_partner)
    down_chip = from_chip(down, weight_partner)
    gate_up_core, down_core = from_core(gate_up), from_core(down)
    gate_up_far = from_core(gate_up_chip)
    down_far = from_core(down_chip)
    other_rows = from_chip(rows, row_partner)
    kept, sent = expert_partials(
        rows,
        other_rows,
        (gate_up, gate_up_core, gate_up_chip, gate_up_far),
        (down, down_core, down_chip, down_far),
    )
    shared_hidden = gated_rows(all_tokens, shared_gate_up)
    shared_part = jnp.dot(shared_hidden, shared_down, preferred_element_type=jnp.float32)
    shared_scale = jax.nn.sigmoid(
        jnp.dot(all_tokens, shared_gate, preferred_element_type=jnp.float32)
    )
    expert_out = kept + from_chip(sent, row_partner).astype(jnp.float32)
    routed = jnp.dot(pick, expert_out.astype(jnp.bfloat16), preferred_element_type=jnp.float32)
    share = shared_scale[:, None] * shared_part + factor * routed
    share = share.reshape(near, planes // near, tok_rows, width)
    return reduce_planes(share, near).astype(jnp.bfloat16)


def solution(mesh):
    in_specs = (
        P(("groups", "plane", "depth", "tok"), None),
        P(("groups", "plane", "depth", "tok"), None),
        P(("groups", "plane", "depth", "tok"), None),
        P(("groups", "plane", "depth", "tok"), None),
        P(),
        P(None, None, "plane"),
        P("plane", None),
        P("plane", None, None, ("depth", "tok")),
        P("plane", ("depth", "tok"), None),
    )
    out_specs = P(("groups", "plane", "depth", "tok"), None)
    return jax.shard_map(
        on_device, mesh=mesh, in_specs=in_specs, out_specs=out_specs, check_vma=False
    )
```

profile of v0, /device:TPU:40, one launch (start us, length us, event | category | flops | bytes accessed | tf_op | source)
XLA Modules:
  0.0 240.6 jit_solution(1906428322266661382)
XLA Ops:
  2.3 73.1 %all-gather = bf16[64,2176]{1,0:T(8,128)(2,1)S(1)} all-gather(bf16[8,2176]{1,0:T(8,128)(2,1)S(1)} %fusion.19), channel_id=2, replica_groups={{0,32,64,96,128,160,192,224},{8,40,72,104,136,168,200,232},{16,48,80,11..., dimensions={0}, use_global_device_ids=true | all-gather | bytes 313344 | tf_op jit(solution)/shard_map/all_gather | solution.py:33
  75.4 9.5 %collective-permute-start.1 = (bf16[8,8,2176]{2,1,0:T(8,128)(2,1)S(1)}, bf16[8,8,2176]{2,1,0:T(8,128)(2,1)S(1)}, u32[]{:S(2)}, u32[]{:S(2)}) collective-permute-start(bf16[8,8,2176]{2,1,0:T(8,128)(2,1)S(1)} %bitcast.50), channel_id=1, source_target_pairs={{16,0},{241,1},{24,8},{249,9},{32,16},{1,17},{40,24},{9,25},{48,32... | collective-permute-start | bytes 835592 | tf_op jit(solution)/shard_map/ppermute | solution.py:19
  84.9 5.1 %collective-permute-start = (bf16[8,8,2176]{2,1,0:T(8,128)(2,1)S(1)}, bf16[8,8,2176]{2,1,0:T(8,128)(2,1)}, u32[]{:S(2)}, u32[]{:S(2)}) collective-permute-start(bf16[8,8,2176]{2,1,0:T(8,128)(2,1)S(1)} %bitcast.51), channel_id=1, source_target_pairs={{8,0},{249,1},{16,8},{1,9},{24,16},{9,17},{32,24},{17,25},{40,32},... | collective-permute-start | bytes 835592 | tf_op jit(solution)/shard_map/ppermute | solution.py:19
  90.0 3.4 %collective-permute-start.2 = (bf16[8,8,2176]{2,1,0:T(8,128)(2,1)S(1)}, bf16[8,8,2176]{2,1,0:T(8,128)(2,1)}, u32[]{:S(2)}, u32[]{:S(2)}) collective-permute-start(bf16[8,8,2176]{2,1,0:T(8,128)(2,1)S(1)} %bitcast.52), channel_id=1, source_target_pairs={{248,0},{9,1},{0,8},{17,9},{8,16},{25,17},{16,24},{33,25},{24,32},... | collective-permute-start | bytes 835592 | tf_op jit(solution)/shard_map/ppermute | solution.py:19
  93.4 3.6 %collective-permute-start.8 = (bf16[176,2048]{1,0:T(8,128)(2,1)}, bf16[176,2048]{1,0:T(8,128)(2,1)S(1)}, u32[]{:S(2)}, u32[]{:S(2)}) collective-permute-start(bf16[176,2048]{1,0:T(8,128)(2,1)} %bitcast.41), channel_id=1, source_target_pairs={{2,0},{0,2},{6,4},{4,6},{3,1},{1,3},{7,5},{5,7},{10,8},{8,10},{14,... | collective-permute-start | bytes 2162696 | tf_op jit(solution)/shard_map/ppermute | solution.py:55
  97.0 2.3 collective-permute-start.5
  100.2 2.0 collective-permute-start.7
  102.2 2.4 %collective-permute-start.4 = (bf16[2,176,2048]{2,1,0:T(8,128)(2,1)}, bf16[2,176,2048]{2,1,0:T(8,128)(2,1)}, u32[]{:S(2)}, u32[]{:S(2)}) collective-permute-start(bf16[2,176,2048]{2,1,0:T(8,128)(2,1)} %bitcast.39), channel_id=1, source_target_pairs={{1,0},{0,1},{3,2},{2,3},{5,4},{4,5},{7,6},{6,7},{9,8},{8,9},{11,10... | collective-permute-start | bytes 4325384 | tf_op jit(solution)/shard_map/ppermute | solution.py:24
  107.0 27.0 %collective-permute-done.5.refs_2_ = bf16[2,176,2048]{2,1,0:T(8,128)(2,1)S(1)} collective-permute-done((bf16[2,176,2048]{2,1,0:T(8,128)(2,1)}, bf16[2,176,2048]{2,1,0:T(8,128)(2,1)S(1)}, u32[]{:S(2)}, u32[]{:S(2)}) %collective-permute-start.5) | collective-permute-done | bytes 1441824 | tf_op jit(solution)/shard_map/ppermute | solution.py:55
  134.0 1.9 collective-permute-start.6
  137.6 1.7 fusion.3
  139.4 2.4 %collective-permute-start.9 = (bf16[176,2048]{1,0:T(8,128)(2,1)S(1)}, bf16[176,2048]{1,0:T(8,128)(2,1)S(1)}, u32[]{:S(2)}, u32[]{:S(2)}) collective-permute-start(bf16[176,2048]{1,0:T(8,128)(2,1)S(1)} %collective-permute-done.8.refs_6_), channel_id=1, source_target_pairs={{1,0},{0,1},{3,2},{2,3},{5,4},{4,5},{7,6},{6,7},{9,8},{8,9},{11,10... | collective-permute-start | bytes 2162696 | tf_op jit(solution)/shard_map/ppermute | solution.py:24
  142.2 5.2 %collective-permute-start.3 = (bf16[64,2048]{1,0:T(8,128)(2,1)S(1)}, bf16[64,2048]{1,0:T(8,128)(2,1)S(1)}, u32[]{:S(2)}, u32[]{:S(2)}) collective-permute-start(bf16[64,2048]{1,0:T(8,128)(2,1)S(1)} %convolution_convert_fusion.own_ref), channel_id=1, source_target_pairs={{6,0},{4,2},{2,4},{0,6},{7,1},{5,3},{3,5},{1,7},{14,8},{12,10},{10... | collective-permute-start | bytes 786440 | tf_op jit(solution)/shard_map/ppermute | solution.py:55
  148.2 5.8 %collective-permute-done.3.other_ref = bf16[64,2048]{1,0:T(8,128)(2,1)S(1)} collective-permute-done((bf16[64,2048]{1,0:T(8,128)(2,1)S(1)}, bf16[64,2048]{1,0:T(8,128)(2,1)S(1)}, u32[]{:S(2)}, u32[]{:S(2)}) %collective-permute-start.3) | collective-permute-done | bytes 262176 | tf_op jit(solution)/shard_map/ppermute | solution.py:55
  154.0 5.0 %shard_map.91 = (f32[64,2048]{1,0:T(8,128)S(1)}, bf16[64,2048]{1,0:T(8,128)(2,1)S(1)}) custom-call(bf16[64,2048]{1,0:T(8,128)(2,1)S(1)} %convolution_convert_fusion.own_ref, bf16[64,2048]{1,0:T(8,128)(2,1)S(1)} %collective-permute-done.3.other_ref, bf16[2,176,2048]{2,1,0:T(8,128)(2,1)S(1)} %bitcast.40, bf16[2,176,2048]{2,1,0:T(8,128)(2,1)} %collective-permute-done.4.refs_1_, ...), custom_call_target="tpu_custom_call" | custom-call | flops 1107296256 | bytes 8650752 | tf_op jit(solution)/shard_map/pallas_call | solution.py:97
  159.0 4.9 %collective-permute-start.10 = (bf16[64,2048]{1,0:T(8,128)(2,1)S(1)}, bf16[64,2048]{1,0:T(8,128)(2,1)S(1)}, u32[]{:S(2)}, u32[]{:S(2)}) collective-permute-start(bf16[64,2048]{1,0:T(8,128)(2,1)S(1)} %get-tuple-element.8), channel_id=1, source_target_pairs={{6,0},{4,2},{2,4},{0,6},{7,1},{5,3},{3,5},{1,7},{14,8},{12,10},{10... | collective-permute-start | bytes 786440 | tf_op jit(solution)/shard_map/ppermute | solution.py:55
  164.4 5.3 %collective-permute-done.10 = bf16[64,2048]{1,0:T(8,128)(2,1)S(1)} collective-permute-done((bf16[64,2048]{1,0:T(8,128)(2,1)S(1)}, bf16[64,2048]{1,0:T(8,128)(2,1)S(1)}, u32[]{:S(2)}, u32[]{:S(2)}) %collective-permute-start.10) | collective-permute-done | bytes 262176 | tf_op jit(solution)/shard_map/ppermute | solution.py:55
  170.3 2.8 %collective-permute-start.11 = (bf16[8,8,2048]{2,1,0:T(8,128)(2,1)S(1)}, bf16[8,8,2048]{2,1,0:T(8,128)(2,1)S(1)}, u32[]{:S(2)}, u32[]{:S(2)}) collective-permute-start(bf16[8,8,2048]{2,1,0:T(8,128)(2,1)S(1)} %get-tuple-element.9), channel_id=1, source_target_pairs={{248,0},{9,1},{0,8},{17,9},{8,16},{25,17},{16,24},{33,25},{24,32},... | collective-permute-start | bytes 786440 | tf_op jit(solution)/shard_map/ppermute | solution.py:19
  173.1 4.3 %collective-permute-start.13 = (bf16[8,8,2048]{2,1,0:T(8,128)(2,1)S(1)}, bf16[8,8,2048]{2,1,0:T(8,128)(2,1)S(1)}, u32[]{:S(2)}, u32[]{:S(2)}) collective-permute-start(bf16[8,8,2048]{2,1,0:T(8,128)(2,1)S(1)} %get-tuple-element.10), channel_id=1, source_target_pairs={{8,0},{249,1},{16,8},{1,9},{24,16},{9,17},{32,24},{17,25},{40,32},... | collective-permute-start | bytes 786440 | tf_op jit(solution)/shard_map/ppermute | solution.py:19
  177.4 2.0 collective-permute-start.12
  179.4 3.0 %collective-permute-done.11 = bf16[8,8,2048]{2,1,0:T(8,128)(2,1)S(1)} collective-permute-done((bf16[8,8,2048]{2,1,0:T(8,128)(2,1)S(1)}, bf16[8,8,2048]{2,1,0:T(8,128)(2,1)S(1)}, u32[]{:S(2)}, u32[]{:S(2)}) %collective-permute-start.11) | collective-permute-done | bytes 262176 | tf_op jit(solution)/shard_map/ppermute | solution.py:19
  182.3 3.5 %collective-permute-done.13 = bf16[8,8,2048]{2,1,0:T(8,128)(2,1)S(1)} collective-permute-done((bf16[8,8,2048]{2,1,0:T(8,128)(2,1)S(1)}, bf16[8,8,2048]{2,1,0:T(8,128)(2,1)S(1)}, u32[]{:S(2)}, u32[]{:S(2)}) %collective-permute-start.13) | collective-permute-done | bytes 262176 | tf_op jit(solution)/shard_map/ppermute | solution.py:19
  185.8 3.5 %collective-permute-done.12 = bf16[8,8,2048]{2,1,0:T(8,128)(2,1)S(1)} collective-permute-done((bf16[8,8,2048]{2,1,0:T(8,128)(2,1)S(1)}, bf16[8,8,2048]{2,1,0:T(8,128)(2,1)S(1)}, u32[]{:S(2)}, u32[]{:S(2)}) %collective-permute-start.12) | collective-permute-done | bytes 262176 | tf_op jit(solution)/shard_map/ppermute | solution.py:19
  189.5 50.5 %all_to_all.5 = bf16[8,8,2048]{2,1,0:T(8,128)(2,1)S(1)} all-to-all(bf16[8,8,2048]{2,1,0:T(8,128)(2,1)S(1)} %fusion.15), channel_id=1, replica_groups={{0,32,64,96,128,160,192,224},{8,40,72,104,136,168,200,232},{16,48,80,11..., dimensions={0} | all-to-all | bytes 524288 | tf_op jit(solution)/shard_map/all_to_all | solution.py:42
  (47 shorter events, 9.9 us)
Async XLA Ops:
  0.0 163.9 %copy-start = (bf16[176,2048]{1,0:T(8,128)(2,1)S(1)}, bf16[176,2048]{1,0:T(8,128)(2,1)}, u32[]{:S(2)}) copy-start(bf16[176,2048]{1,0:T(8,128)(2,1)} %param.15) | copy-start | bytes 2162692
  75.4 24.8 %collective-permute-start.1 = (bf16[8,8,2176]{2,1,0:T(8,128)(2,1)S(1)}, bf16[8,8,2176]{2,1,0:T(8,128)(2,1)S(1)}, u32[]{:S(2)}, u32[]{:S(2)}) collective-permute-start(bf16[8,8,2176]{2,1,0:T(8,128)(2,1)S(1)} %bitcast.50), channel_id=1, source_target_pairs={{16,0},{241,1},{24,8},{249,9},{32,16},{1,17},{40,24},{9,25},{48,32... | collective-permute-start | bytes 835592 | tf_op jit(solution)/shard_map/ppermute | solution.py:19
  84.9 17.2 %collective-permute-start = (bf16[8,8,2176]{2,1,0:T(8,128)(2,1)S(1)}, bf16[8,8,2176]{2,1,0:T(8,128)(2,1)}, u32[]{:S(2)}, u32[]{:S(2)}) collective-permute-start(bf16[8,8,2176]{2,1,0:T(8,128)(2,1)S(1)} %bitcast.51), channel_id=1, source_target_pairs={{8,0},{249,1},{16,8},{1,9},{24,16},{9,17},{32,24},{17,25},{40,32},... | collective-permute-start | bytes 835592 | tf_op jit(solution)/shard_map/ppermute | solution.py:19
  90.0 14.6 %collective-permute-start.2 = (bf16[8,8,2176]{2,1,0:T(8,128)(2,1)S(1)}, bf16[8,8,2176]{2,1,0:T(8,128)(2,1)}, u32[]{:S(2)}, u32[]{:S(2)}) collective-permute-start(bf16[8,8,2176]{2,1,0:T(8,128)(2,1)S(1)} %bitcast.52), channel_id=1, source_target_pairs={{248,0},{9,1},{0,8},{17,9},{8,16},{25,17},{16,24},{33,25},{24,32},... | collective-permute-start | bytes 835592 | tf_op jit(solution)/shard_map/ppermute | solution.py:19
  93.4 46.0 %collective-permute-start.8 = (bf16[176,2048]{1,0:T(8,128)(2,1)}, bf16[176,2048]{1,0:T(8,128)(2,1)S(1)}, u32[]{:S(2)}, u32[]{:S(2)}) collective-permute-start(bf16[176,2048]{1,0:T(8,128)(2,1)} %bitcast.41), channel_id=1, source_target_pairs={{2,0},{0,2},{6,4},{4,6},{3,1},{1,3},{7,5},{5,7},{10,8},{8,10},{14,... | collective-permute-start | bytes 2162696 | tf_op jit(solution)/shard_map/ppermute | solution.py:55
  97.0 37.1 %collective-permute-start.5 = (bf16[2,176,2048]{2,1,0:T(8,128)(2,1)}, bf16[2,176,2048]{2,1,0:T(8,128)(2,1)S(1)}, u32[]{:S(2)}, u32[]{:S(2)}) collective-permute-start(bf16[2,176,2048]{2,1,0:T(8,128)(2,1)} %bitcast.38), channel_id=1, source_target_pairs={{2,0},{0,2},{6,4},{4,6},{3,1},{1,3},{7,5},{5,7},{10,8},{8,10},{14,... | collective-permute-start | bytes 4325384 | tf_op jit(solution)/shard_map/ppermute | solution.py:55
  100.2 53.7 %collective-permute-start.7 = (bf16[176,2048]{1,0:T(8,128)(2,1)}, bf16[176,2048]{1,0:T(8,128)(2,1)}, u32[]{:S(2)}, u32[]{:S(2)}) collective-permute-start(bf16[176,2048]{1,0:T(8,128)(2,1)} %bitcast.42), channel_id=1, source_target_pairs={{1,0},{0,1},{3,2},{2,3},{5,4},{4,5},{7,6},{6,7},{9,8},{8,9},{11,10... | collective-permute-start | bytes 2162696 | tf_op jit(solution)/shard_map/ppermute | solution.py:24
  102.2 51.7 %collective-permute-start.4 = (bf16[2,176,2048]{2,1,0:T(8,128)(2,1)}, bf16[2,176,2048]{2,1,0:T(8,128)(2,1)}, u32[]{:S(2)}, u32[]{:S(2)}) collective-permute-start(bf16[2,176,2048]{2,1,0:T(8,128)(2,1)} %bitcast.39), channel_id=1, source_target_pairs={{1,0},{0,1},{3,2},{2,3},{5,4},{4,5},{7,6},{6,7},{9,8},{8,9},{11,10... | collective-permute-start | bytes 4325384 | tf_op jit(solution)/shard_map/ppermute | solution.py:24
  105.9 1.0 copy-start.3
  106.9 30.7 %copy-start.4 = (bf16[4,8,8,2176]{3,2,1,0:T(8,128)(2,1)S(1)}, bf16[4,8,8,2176]{3,2,1,0:T(8,128)(2,1)}, u32[]{:S(2)}) copy-start(bf16[4,8,8,2176]{3,2,1,0:T(8,128)(2,1)} %copy-done.3) | copy-start | bytes 3342340
  134.0 19.9 %collective-permute-start.6 = (bf16[2,176,2048]{2,1,0:T(8,128)(2,1)S(1)}, bf16[2,176,2048]{2,1,0:T(8,128)(2,1)S(1)}, u32[]{:S(2)}, u32[]{:S(2)}) collective-permute-start(bf16[2,176,2048]{2,1,0:T(8,128)(2,1)S(1)} %collective-permute-done.5.refs_2_), channel_id=1, source_target_pairs={{1,0},{0,1},{3,2},{2,3},{5,4},{4,5},{7,6},{6,7},{9,8},{8,9},{11,10... | collective-permute-start | bytes 4325384 | tf_op jit(solution)/shard_map/ppermute | solution.py:24
  137.6 9.8 %copy-start.5 = (bf16[2,2048,176]{1,2,0:T(8,128)(2,1)S(1)}, bf16[2,2048,176]{1,2,0:T(8,128)(2,1)}, u32[]{:S(2)}) copy-start(bf16[2,2048,176]{1,2,0:T(8,128)(2,1)} %param.14) | copy-start | bytes 4325380
  139.4 14.5 %collective-permute-start.9 = (bf16[176,2048]{1,0:T(8,128)(2,1)S(1)}, bf16[176,2048]{1,0:T(8,128)(2,1)S(1)}, u32[]{:S(2)}, u32[]{:S(2)}) collective-permute-start(bf16[176,2048]{1,0:T(8,128)(2,1)S(1)} %collective-permute-done.8.refs_6_), channel_id=1, source_target_pairs={{1,0},{0,1},{3,2},{2,3},{5,4},{4,5},{7,6},{6,7},{9,8},{8,9},{11,10... | collective-permute-start | bytes 2162696 | tf_op jit(solution)/shard_map/ppermute | solution.py:24
  142.2 11.7 %copy-start.1 = (bf16[1,2,2048,176]{2,3,1,0:T(8,128)(2,1)S(1)}, bf16[1,2,2048,176]{2,3,1,0:T(8,128)(2,1)}, u32[]{:S(2)}) copy-start(bf16[1,2,2048,176]{2,3,1,0:T(8,128)(2,1)} %param.16) | copy-start | bytes 4325380
  142.2 11.8 %copy-start.2 = (bf16[1,176,2048]{2,1,0:T(8,128)(2,1)S(1)}, bf16[1,176,2048]{2,1,0:T(8,128)(2,1)}, u32[]{:S(2)}) copy-start(bf16[1,176,2048]{2,1,0:T(8,128)(2,1)} %param.17) | copy-start | bytes 2162692
  142.2 11.7 %collective-permute-start.3 = (bf16[64,2048]{1,0:T(8,128)(2,1)S(1)}, bf16[64,2048]{1,0:T(8,128)(2,1)S(1)}, u32[]{:S(2)}, u32[]{:S(2)}) collective-permute-start(bf16[64,2048]{1,0:T(8,128)(2,1)S(1)} %convolution_convert_fusion.own_ref), channel_id=1, source_target_pairs={{6,0},{4,2},{2,4},{0,6},{7,1},{5,3},{3,5},{1,7},{14,8},{12,10},{10... | collective-permute-start | bytes 786440 | tf_op jit(solution)/shard_map/ppermute | solution.py:55
  159.0 10.7 %collective-permute-start.10 = (bf16[64,2048]{1,0:T(8,128)(2,1)S(1)}, bf16[64,2048]{1,0:T(8,128)(2,1)S(1)}, u32[]{:S(2)}, u32[]{:S(2)}) collective-permute-start(bf16[64,2048]{1,0:T(8,128)(2,1)S(1)} %get-tuple-element.8), channel_id=1, source_target_pairs={{6,0},{4,2},{2,4},{0,6},{7,1},{5,3},{3,5},{1,7},{14,8},{12,10},{10... | collective-permute-start | bytes 786440 | tf_op jit(solution)/shard_map/ppermute | solution.py:55
  170.3 12.0 %collective-permute-start.11 = (bf16[8,8,2048]{2,1,0:T(8,128)(2,1)S(1)}, bf16[8,8,2048]{2,1,0:T(8,128)(2,1)S(1)}, u32[]{:S(2)}, u32[]{:S(2)}) collective-permute-start(bf16[8,8,2048]{2,1,0:T(8,128)(2,1)S(1)} %get-tuple-element.9), channel_id=1, source_target_pairs={{248,0},{9,1},{0,8},{17,9},{8,16},{25,17},{16,24},{33,25},{24,32},... | collective-permute-start | bytes 786440 | tf_op jit(solution)/shard_map/ppermute | solution.py:19
  173.1 12.8 %collective-permute-start.13 = (bf16[8,8,2048]{2,1,0:T(8,128)(2,1)S(1)}, bf16[8,8,2048]{2,1,0:T(8,128)(2,1)S(1)}, u32[]{:S(2)}, u32[]{:S(2)}) collective-permute-start(bf16[8,8,2048]{2,1,0:T(8,128)(2,1)S(1)} %get-tuple-element.10), channel_id=1, source_target_pairs={{8,0},{249,1},{16,8},{1,9},{24,16},{9,17},{32,24},{17,25},{40,32},... | collective-permute-start | bytes 786440 | tf_op jit(solution)/shard_map/ppermute | solution.py:19
  177.4 12.0 %collective-permute-start.12 = (bf16[8,8,2048]{2,1,0:T(8,128)(2,1)S(1)}, bf16[8,8,2048]{2,1,0:T(8,128)(2,1)S(1)}, u32[]{:S(2)}, u32[]{:S(2)}) collective-permute-start(bf16[8,8,2048]{2,1,0:T(8,128)(2,1)S(1)} %get-tuple-element.11), channel_id=1, source_target_pairs={{240,0},{17,1},{248,8},{25,9},{0,16},{33,17},{8,24},{41,25},{16,32... | collective-permute-start | bytes 786440 | tf_op jit(solution)/shard_map/ppermute | solution.py:19
where the time goes:
time: 241 us
  blocking collectives  124 us (51%)
  starting transfers between devices  51.8 us (21%)
  waiting for transfers between devices  48.2 us (20%)
  Pallas kernels  5.04 us (2%)
  matrix products  5.03 us (2%)
  other arithmetic  4.68 us (2%)
    all_gather x1, blocking collectives, gather_planes(): own = lax.all_gather(block, 'plane', axis_index_groups=groups)  73.1 us
    all_to_all x1, blocking collectives, reduce_planes(): lax.all_to_all(total.astype(jnp.bfloat16), 'plane', split_axis=0, concat_...  50.5 us
    ppermute x4, waiting for transfers between devices, from_chip(): lax.ppermute(block, 'depth', [(partner(i, size), i) for i in range(size)])  38.1 us
    ppermute x6, starting transfers between devices, from_offset(): return lax.ppermute(block, (axis, 'tok'), pairs)  27 us
    ppermute x4, starting transfers between devices, from_chip(): lax.ppermute(block, 'depth', [(partner(i, size), i) for i in range(size)])  16 us
    ppermute x6, waiting for transfers between devices, from_offset(): return lax.ppermute(block, (axis, 'tok'), pairs)  10 us
    ppermute x4, starting transfers between devices, from_core(): lax.ppermute(block, 'tok', [((i + 1) % size, i) for i in range(size)])  8.77 us
    pallas_call x1, Pallas kernels, expert_partials(): pl.pallas_call(expert_kernel, out_shape=(jax.ShapeDtypeStruct((rows, widt...  5.04 us
  transfers between devices with their start and end apart: 14, of which 6 were waited for; matrix products, arithmetic and copies ran while one was open for 3% of the time, Pallas kernels for 0%

commit v1 on v0

--- a/solution.py
+++ b/solution.py
@@ -1,3 +1,5 @@
+import functools
+
 import jax
 import jax.numpy as jnp
 from jax import lax
@@ -7,6 +9,7 @@
 
 LANES = 128
 KERNEL_VMEM = 14 << 20
+GLUE_VMEM = 10 << 20
 
 
 def from_offset(block, axis, offset):
@@ -30,17 +33,16 @@
 
 def gather_planes(block, near):
     groups = far_groups(lax.axis_size("plane"), near)
-    own = lax.all_gather(block, "plane", axis_index_groups=groups)
-    return jnp.stack([own] + [from_offset(own, "plane", k) for k in (1, 2, -1)])
-
-
-def reduce_planes(blocks, near):
-    sent = blocks.astype(jnp.bfloat16)
-    total = blocks[0]
-    for j, k in ((1, 1), (2, 2), (3, -1)):
-        total = total + from_offset(sent[j], "plane", -k).astype(jnp.float32)
+    own = lax.all_gather(block, "plane", axis_index_groups=groups, tiled=True)
+    return [own] + [from_offset(own, "plane", k) for k in (1, 2, -1)]
+
+
+def reduce_planes(own, sent, near, rows):
+    total = own
+    for block, k in zip(sent, (1, 2, -1)):
+        total = total + from_offset(block, "plane", -k).astype(jnp.float32)
     arrived = lax.all_to_all(
-        total.astype(jnp.bfloat16),
+        total.astype(jnp.bfloat16).reshape(-1, rows, total.shape[1]),
         "plane",
         split_axis=0,
         concat_axis=0,
@@ -116,10 +118,93 @@
     )(own, other, *gate_ups, *downs)
 
 
-def gated_rows(token_rows, gate_up):
-    gate_part = jnp.dot(token_rows, gate_up[0], preferred_element_type=jnp.float32)
-    up_part = jnp.dot(token_rows, gate_up[1], preferred_element_type=jnp.float32)
-    return lax.optimization_barrier((jax.nn.silu(gate_part) * up_part).astype(jnp.bfloat16))
+def notes_kernel(tokens_hbm, *refs, capacity):
+    sources, out_ref, (ids_ref, slots_ref, weights_ref), sems = refs[:3], refs[3], refs[4:7], refs[7]
+    width = tokens_hbm.shape[1]
+    choices, rows = ids_ref.shape
+    targets = (ids_ref, slots_ref, weights_ref)
+    copies = [pltpu.make_async_copy(a, b, sems.at[i]) for i, (a, b) in enumerate(zip(sources, targets))]
+    copies.append(pltpu.make_async_copy(tokens_hbm, out_ref.at[:, pl.ds(0, width)], sems.at[3]))
+    for copy in copies:
+        copy.start()
+    for copy in copies[:3]:
+        copy.wait()
+    slots = slots_ref[...]
+    code = jnp.where(slots < capacity, ids_ref[...] * capacity + slots, -1).astype(jnp.float32)
+    notes = jnp.concatenate([code, weights_ref[...].astype(jnp.float32)])
+    lane = lax.broadcasted_iota(jnp.int32, (rows, LANES), 1)
+    row = lax.broadcasted_iota(jnp.int32, (rows, rows), 0)
+    column = lax.broadcasted_iota(jnp.int32, (rows, rows), 1)
+    placed = jnp.zeros((rows, LANES), jnp.float32)
+    for k in range(2 * choices):
+        spread = jnp.where(row == column, notes[k : k + 1, :], 0.0)
+        value = jnp.sum(spread, axis=1, keepdims=True)
+        placed = jnp.where(lane == k, value, placed)
+    out_ref[:, width:] = placed.astype(jnp.bfloat16)
+    copies[3].wait()
+
+
+def picks_kernel(first_ref, *refs, capacity, choices, tok_rows):
+    blocks, (rows_ref, mix_ref) = refs[:-2], refs[-2:]
+    count, width = blocks[0].shape[0], rows_ref.shape[1]
+    slots = mix_ref.shape[2]
+    token = lax.broadcasted_iota(jnp.int32, (count, slots), 0)
+    slot = lax.broadcasted_iota(jnp.int32, (count, slots), 1)
+    wanted = (first_ref[0] + slot % capacity).astype(jnp.float32)
+    here = slot // capacity == token // tok_rows
+    for j, block in enumerate(blocks):
+        notes = block[:, width:].astype(jnp.float32)
+        weight = jnp.zeros((count, slots), jnp.float32)
+        found = jnp.zeros((count, slots), jnp.float32)
+        for k in range(choices):
+            match = here & (notes[:, k : k + 1] == wanted)
+            found = jnp.where(match, 1.0, found)
+            weight = jnp.where(match, notes[:, choices + k : choices + k + 1], weight)
+        rows = lax.dot_general(
+            found.astype(jnp.bfloat16),
+            block[:, :width],
+            (((0,), (0,)), ((), ())),
+            preferred_element_type=jnp.float32,
+        )
+        rows_ref[j * slots : (j + 1) * slots, :] = rows.astype(jnp.bfloat16)
+        mix_ref[j] = weight.astype(jnp.bfloat16)
+
+
+def shared_kernel(*refs):
+    blocks, (gate_ref, gate_up_hbm, down_hbm, out_ref, gate_up, down, sems) = refs[:-7], refs[-7:]
+    fetch_in = pltpu.make_async_copy(gate_up_hbm, gate_up, sems.at[0])
+    fetch_out = pltpu.make_async_copy(down_hbm, down, sems.at[1])
+    fetch_in.start()
+    fetch_out.start()
+    count, width = blocks[0].shape[0], out_ref.shape[2]
+    gate_row = gate_ref[...].astype(jnp.float32)
+    scales = []
+    for block in blocks:
+        score = jnp.sum(block[:, :width].astype(jnp.float32) * gate_row, axis=1, keepdims=True)
+        scales.append(1.0 / (1.0 + jnp.exp(-score)))
+    tokens = jnp.concatenate([block[:, :width] for block in blocks])
+    contract = (((1,), (1,)), ((), ()))
+    fetch_in.wait()
+    gate = lax.dot_general(tokens, gate_up[0], contract, preferred_element_type=jnp.float32)
+    up = lax.dot_general(tokens, gate_up[1], contract, preferred_element_type=jnp.float32)
+    hidden = (gate / (1.0 + jnp.exp(-gate)) * up).astype(jnp.bfloat16)
+    fetch_out.wait()
+    for j, scale in enumerate(scales):
+        part = hidden[j * count : (j + 1) * count]
+        out_ref[j] = scale * jnp.dot(part, down[...], preferred_element_type=jnp.float32)
+
+
+def combine_kernel(kept_ref, got_ref, mix_ref, shared_ref, own_ref, *sent_refs):
+    rows = (kept_ref[...] + got_ref[...].astype(jnp.float32)).astype(jnp.bfloat16)
+    slots = mix_ref.shape[2]
+    for j, out_ref in enumerate((own_ref, *sent_refs)):
+        part = rows[j * slots : (j + 1) * slots]
+        routed = jnp.dot(mix_ref[j], part, preferred_element_type=jnp.float32)
+        out_ref[...] = (shared_ref[j] + routed).astype(out_ref.dtype)
+
+
+def in_vmem(count):
+    return [pl.BlockSpec(memory_space=pltpu.VMEM)] * count
 
 
 def on_device(
@@ -138,31 +223,41 @@
     choices = expert_ids.shape[1]
     capacity = max(2, tok_rows * choices // planes)
     near = 4
-    slots = planes * capacity
-
-    code = jnp.where(slot_index < capacity, expert_ids * capacity + slot_index, -1)
-    notes = jnp.concatenate([code.astype(jnp.bfloat16), route_weight], axis=1)
-    notes = jnp.pad(notes, ((0, 0), (0, LANES - 2 * choices)))
-    gathered = gather_planes(jnp.concatenate([tokens, notes], axis=1), near)
-    gathered = gathered.reshape(planes * tok_rows, width + LANES)
-    all_tokens = gathered[:, :width]
-    codes = gathered[:, width : width + choices].astype(jnp.float32)
-    weights = gathered[:, width + choices : width + 2 * choices].astype(jnp.float32)
-
-    mine = (lax.axis_index("plane") * capacity).astype(jnp.float32)
-    count = planes * tok_rows
-    here = lax.broadcasted_iota(jnp.int32, (count, slots), 0) // tok_rows
-    column = lax.broadcasted_iota(jnp.int32, (count, slots), 1)
-    slot_code = mine + (column % capacity).astype(jnp.float32)
-    hit = jnp.any(codes[:, None, :] == slot_code[:, :, None], axis=2)
-    pick = (hit & (here == column // capacity)).astype(jnp.bfloat16)
-    pick = lax.optimization_barrier(pick)
-    matched = (codes >= mine) & (codes < mine + capacity)
-    factor = jnp.sum(jnp.where(matched, weights, 0.0), axis=1, keepdims=True)
-
-    rows = lax.dot_general(
-        pick, all_tokens, (((0,), (0,)), ((), ())), preferred_element_type=jnp.float32
-    ).astype(jnp.bfloat16)
+    count = planes // near * tok_rows
+    slots = planes // near * capacity
+    units = shared_down.shape[0]
+    anywhere = pl.BlockSpec(memory_space=pl.ANY)
+    small = pltpu.CompilerParams(vmem_limit_bytes=GLUE_VMEM)
+
+    noted = pl.pallas_call(
+        functools.partial(notes_kernel, capacity=capacity),
+        out_shape=jax.ShapeDtypeStruct((tok_rows, width + LANES), jnp.bfloat16),
+        in_specs=[pl.BlockSpec(memory_space=pltpu.HBM)] * 4,
+        out_specs=in_vmem(1)[0],
+        scratch_shapes=[
+            pltpu.VMEM((choices, tok_rows), jnp.int32),
+            pltpu.VMEM((choices, tok_rows), jnp.int32),
+            pltpu.VMEM((choices, tok_rows), jnp.bfloat16),
+            pltpu.SemaphoreType.DMA((4,)),
+        ],
+        compiler_params=pltpu.CompilerParams(vmem_limit_bytes=64 << 20),
+    )(tokens, expert_ids.T, slot_index.T, route_weight.T)
+    blocks = gather_planes(noted, near)
+
+    first = (lax.axis_index("plane") * capacity).astype(jnp.int32).reshape(1)
+    rows, mix = pl.pallas_call(
+        functools.partial(
+            picks_kernel, capacity=capacity, choices=choices, tok_rows=tok_rows
+        ),
+        out_shape=(
+            jax.ShapeDtypeStruct((near * slots, width), jnp.bfloat16),
+            jax.ShapeDtypeStruct((near, count, slots), jnp.bfloat16),
+        ),
+        in_specs=[pl.BlockSpec(memory_space=pltpu.SMEM)] + in_vmem(near),
+        out_specs=tuple(in_vmem(2)),
+        compiler_params=small,
+    )(first, *blocks)
+
     gate_up, down = expert_gate_up[0].swapaxes(1, 2), expert_down[0]
     gate_up_chip = from_chip(gate_up, weight_partner)
     down_chip = from_chip(down, weight_partner)
@@ -176,16 +271,35 @@
         (gate_up, gate_up_core, gate_up_chip, gate_up_far),
         (down, down_core, down_chip, down_far),
     )
-    shared_hidden = gated_rows(all_tokens, shared_gate_up)
-    shared_part = jnp.dot(shared_hidden, shared_down, preferred_element_type=jnp.float32)
-    shared_scale = jax.nn.sigmoid(
-        jnp.dot(all_tokens, shared_gate, preferred_element_type=jnp.float32)
-    )
-    expert_out = kept + from_chip(sent, row_partner).astype(jnp.float32)
-    routed = jnp.dot(pick, expert_out.astype(jnp.bfloat16), preferred_element_type=jnp.float32)
-    share = shared_scale[:, None] * shared_part + factor * routed
-    share = share.reshape(near, planes // near, tok_rows, width)
-    return reduce_planes(share, near).astype(jnp.bfloat16)
+    got = from_chip(sent, row_partner)
+
+    shared_part = pl.pallas_call(
+        shared_kernel,
+        out_shape=jax.ShapeDtypeStruct((near, count, width), jnp.float32),
+        in_specs=in_vmem(near + 1) + [anywhere] * 2,
+        out_specs=in_vmem(1)[0],
+        scratch_shapes=[
+            pltpu.VMEM((2, units, width), jnp.bfloat16),
+            pltpu.VMEM((units, width), jnp.bfloat16),
+            pltpu.SemaphoreType.DMA((2,)),
+        ],
+        compiler_params=pltpu.CompilerParams(vmem_limit_bytes=KERNEL_VMEM),
+        cost_estimate=pl.CostEstimate(
+            flops=6 * near * count * width * units,
+            bytes_accessed=6 * units * width,
+            transcendentals=near * count * units,
+        ),
+    )(*blocks, shared_gate.reshape(1, width), shared_gate_up.swapaxes(1, 2), shared_down)
+
+    own, *others = pl.pallas_call(
+        combine_kernel,
+        out_shape=[jax.ShapeDtypeStruct((count, width), jnp.float32)]
+        + [jax.ShapeDtypeStruct((count, width), jnp.bfloat16)] * (near - 1),
+        in_specs=in_vmem(4),
+        out_specs=in_vmem(near),
+        compiler_params=small,
+    )(kept, got, mix, shared_part)
+    return reduce_planes(own, others, near, tok_rows).astype(jnp.bfloat16)
 
 
 def solution(mesh):
@@ -201,6 +315,4 @@
         P("plane", ("depth", "tok"), None),
     )
     out_specs = P(("groups", "plane", "depth", "tok"), None)
-    return jax.shard_map(
-        on_device, mesh=mesh, in_specs=in_specs, out_specs=out_specs, check_vma=False
-    )
+    return jax.shard_map(on_device, mesh=mesh, in_specs=in_specs, out_specs=out_specs, check_vma=False)

time: 241 us -> 242 us (level)
  waiting for transfers between devices: 48.2 us -> 55.5 us
  matrix products: 5.03 us -> 0 us
  Pallas kernels: 5.04 us -> 9.36 us
  other arithmetic: 4.68 us -> 0.77 us
  starting transfers between devices: 51.8 us -> 48.8 us
    ppermute x6, waiting for transfers between devices: 10 us -> 20.2 us  [from_offset(): return lax.ppermute(block, (axis, 'tok'), pairs)]
    dot_general x6 -> x0, matrix products: 5.03 us -> none  [the longest x1 1.72 us: gated_rows(): jnp.dot(token_rows, gate_up[0], preferred_element_type=jnp.float32)]
    pallas_call x0 -> x4, Pallas kernels: none -> 4.66 us  [the longest x1 2.32 us: on_device(): pl.pallas_call(shared_kernel, out_shape=jax.ShapeDtypeStruct((near, count...]
    ppermute x4, waiting for transfers between devices: 38.1 us -> 35.2 us  [from_chip(): lax.ppermute(block, 'depth', [(partner(i, size), i) for i in range(size)])]
    ppermute x6, starting transfers between devices: 27 us -> 24.4 us  [from_offset(): return lax.ppermute(block, (axis, 'tok'), pairs)]
  transfers between devices with their start and end apart: 14 -> 14, of which waited for: 6 -> 8; matrix products, arithmetic and copies ran while one was open for 3% -> 0% of each run, Pallas kernels for 0% -> 2%
where the time goes in v1:
time: 242 us; the launch traced here: 241 us
  blocking collectives  125 us (52%)
  waiting for transfers between devices  55.5 us (23%)
  starting transfers between devices  48.8 us (20%)
  Pallas kernels  9.36 us (4%)
    all_gather x1, blocking collectives, gather_planes(): own = lax.all_gather(block, 'plane', axis_index_groups=groups, tiled=True)  73.6 us
    all_to_all x1, blocking collectives, reduce_planes(): lax.all_to_all(total.astype(jnp.bfloat16).reshape(-1, rows, total.shape[1...  51.4 us
    ppermute x4, waiting for transfers between devices, from_chip(): lax.ppermute(block, 'depth', [(partner(i, size), i) for i in range(size)])  35.2 us
    ppermute x6, starting transfers between devices, from_offset(): return lax.ppermute(block, (axis, 'tok'), pairs)  24.4 us
    ppermute x6, waiting for transfers between devices, from_offset(): return lax.ppermute(block, (axis, 'tok'), pairs)  20.2 us
    ppermute x4, starting transfers between devices, from_chip(): lax.ppermute(block, 'depth', [(partner(i, size), i) for i in range(size)])  16.1 us
    ppermute x4, starting transfers between devices, from_core(): lax.ppermute(block, 'tok', [((i + 1) % size, i) for i in range(size)])  8.27 us
  transfers between devices with their start and end apart: 14, of which 8 were waited for; matrix products, arithmetic and copies ran while one was open for 0% of the time, Pallas kernels for 2%

profile of v1, /device:TPU:40, one launch (start us, length us, event | category | flops | bytes accessed | tf_op | source)
XLA Modules:
  0.0 241.1 jit_solution(12188447866652772631)
XLA Ops:
  0.0 3.6 %collective-permute-start.5 = (bf16[2,176,2048]{2,1,0:T(8,128)(2,1)}, bf16[2,176,2048]{2,1,0:T(8,128)(2,1)}, u32[]{:S(2)}, u32[]{:S(2)}) collective-permute-start(bf16[2,176,2048]{2,1,0:T(8,128)(2,1)} %bitcast.11), channel_id=1, source_target_pairs={{2,0},{0,2},{6,4},{4,6},{3,1},{1,3},{7,5},{5,7},{10,8},{8,10},{14,... | collective-permute-start | bytes 4325384 | tf_op jit(solution)/shard_map/ppermute | solution.py:57
  3.6 2.3 collective-permute-start.8
  5.9 2.0 collective-permute-start.4
  7.9 28.8 %collective-permute-done.5.refs_2_ = bf16[2,176,2048]{2,1,0:T(8,128)(2,1)} collective-permute-done((bf16[2,176,2048]{2,1,0:T(8,128)(2,1)}, bf16[2,176,2048]{2,1,0:T(8,128)(2,1)}, u32[]{:S(2)}, u32[]{:S(2)}) %collective-permute-start.5) | collective-permute-done | bytes 1441824 | tf_op jit(solution)/shard_map/ppermute | solution.py:57
  36.7 1.9 collective-permute-start.6
  40.1 73.6 %all_gather.3.refs_0_ = bf16[64,2176]{1,0:T(8,128)(2,1)S(1)} all-gather(bf16[8,2176]{1,0:T(8,128)(2,1)} %shard_map.91), channel_id=1, replica_groups={{0,32,64,96,128,160,192,224},{8,40,72,104,136,168,200,232},{16,48,80,11..., dimensions={0}, use_global_device_ids=true | all-gather | bytes 313344 | tf_op jit(solution)/shard_map/all_gather | solution.py:36
  113.7 10.4 %collective-permute-start = (bf16[64,2176]{1,0:T(8,128)(2,1)S(1)}, bf16[64,2176]{1,0:T(8,128)(2,1)S(1)}, u32[]{:S(2)}, u32[]{:S(2)}) collective-permute-start(bf16[64,2176]{1,0:T(8,128)(2,1)S(1)} %all_gather.3.refs_0_), channel_id=1, source_target_pairs={{8,0},{249,1},{16,8},{1,9},{24,16},{9,17},{32,24},{17,25},{40,32},... | collective-permute-start | bytes 835592 | tf_op jit(solution)/shard_map/ppermute | solution.py:22
  124.2 2.0 collective-permute-start.1
  126.1 2.2 collective-permute-done.refs_1_
  128.3 1.9 collective-permute-start.7
  130.3 2.4 %collective-permute-start.9 = (bf16[176,2048]{1,0:T(8,128)(2,1)}, bf16[176,2048]{1,0:T(8,128)(2,1)S(1)}, u32[]{:S(2)}, u32[]{:S(2)}) collective-permute-start(bf16[176,2048]{1,0:T(8,128)(2,1)} %collective-permute-done.8.refs_6_), channel_id=1, source_target_pairs={{1,0},{0,1},{3,2},{2,3},{5,4},{4,5},{7,6},{6,7},{9,8},{8,9},{11,10... | collective-permute-start | bytes 2162696 | tf_op jit(solution)/shard_map/ppermute | solution.py:27
  133.6 3.0 %collective-permute-start.2 = (bf16[64,2176]{1,0:T(8,128)(2,1)S(1)}, bf16[64,2176]{1,0:T(8,128)(2,1)S(1)}, u32[]{:S(2)}, u32[]{:S(2)}) collective-permute-start(bf16[64,2176]{1,0:T(8,128)(2,1)S(1)} %all_gather.3.refs_0_), channel_id=1, source_target_pairs={{248,0},{9,1},{0,8},{17,9},{8,16},{25,17},{16,24},{33,25},{24,32},... | collective-permute-start | bytes 835592 | tf_op jit(solution)/shard_map/ppermute | solution.py:22
  136.6 7.7 %collective-permute-done.2.refs_3_ = bf16[64,2176]{1,0:T(8,128)(2,1)S(1)} collective-permute-done((bf16[64,2176]{1,0:T(8,128)(2,1)S(1)}, bf16[64,2176]{1,0:T(8,128)(2,1)S(1)}, u32[]{:S(2)}, u32[]{:S(2)}) %collective-permute-start.2) | collective-permute-done | bytes 278560 | tf_op jit(solution)/shard_map/ppermute | solution.py:22
  144.8 5.1 %collective-permute-start.3 = (bf16[64,2048]{1,0:T(8,128)(2,1)S(1)}, bf16[64,2048]{1,0:T(8,128)(2,1)S(1)}, u32[]{:S(2)}, u32[]{:S(2)}) collective-permute-start(bf16[64,2048]{1,0:T(8,128)(2,1)S(1)} %get-tuple-element.13.own_ref), channel_id=1, source_target_pairs={{6,0},{4,2},{2,4},{0,6},{7,1},{5,3},{3,5},{1,7},{14,8},{12,10},{10... | collective-permute-start | bytes 786440 | tf_op jit(solution)/shard_map/ppermute | solution.py:57
  149.9 4.4 %collective-permute-done.3.other_ref = bf16[64,2048]{1,0:T(8,128)(2,1)S(1)} collective-permute-done((bf16[64,2048]{1,0:T(8,128)(2,1)S(1)}, bf16[64,2048]{1,0:T(8,128)(2,1)S(1)}, u32[]{:S(2)}, u32[]{:S(2)}) %collective-permute-start.3) | collective-permute-done | bytes 262176 | tf_op jit(solution)/shard_map/ppermute | solution.py:57
  155.7 4.7 %shard_map.93 = (f32[64,2048]{1,0:T(8,128)S(1)}, bf16[64,2048]{1,0:T(8,128)(2,1)S(1)}) custom-call(bf16[64,2048]{1,0:T(8,128)(2,1)S(1)} %get-tuple-element.13.own_ref, bf16[64,2048]{1,0:T(8,128)(2,1)S(1)} %collective-permute-done.3.other_ref, bf16[2,176,2048]{2,1,0:T(8,128)(2,1)S(1)} %bitcast.13, bf16[2,176,2048]{2,1,0:T(8,128)(2,1)} %collective-permute-done.4.refs_1_, ...), custom_call_target="tpu_custom_call" | custom-call | flops 1107296256 | bytes 8650752 | tf_op jit(solution)/shard_map/pallas_call | solution.py:99
  160.4 5.1 %collective-permute-start.10 = (bf16[64,2048]{1,0:T(8,128)(2,1)S(1)}, bf16[64,2048]{1,0:T(8,128)(2,1)S(1)}, u32[]{:S(2)}, u32[]{:S(2)}) collective-permute-start(bf16[64,2048]{1,0:T(8,128)(2,1)S(1)} %get-tuple-element.15), channel_id=1, source_target_pairs={{6,0},{4,2},{2,4},{0,6},{7,1},{5,3},{3,5},{1,7},{14,8},{12,10},{10... | collective-permute-start | bytes 786440 | tf_op jit(solution)/shard_map/ppermute | solution.py:57
  165.6 2.3 shard_map.94.shared_ref
  167.9 2.0 collective-permute-done.10.got_ref
  170.3 2.0 collective-permute-start.11
  172.3 2.0 collective-permute-start.12
  174.2 5.2 %collective-permute-start.13 = (bf16[64,2048]{1,0:T(8,128)(2,1)S(1)}, bf16[64,2048]{1,0:T(8,128)(2,1)S(1)}, u32[]{:S(2)}, u32[]{:S(2)}) collective-permute-start(bf16[64,2048]{1,0:T(8,128)(2,1)S(1)} %get-tuple-element.20), channel_id=1, source_target_pairs={{8,0},{249,1},{16,8},{1,9},{24,16},{9,17},{32,24},{17,25},{40,32},... | collective-permute-start | bytes 786440 | tf_op jit(solution)/shard_map/ppermute | solution.py:22
  180.6 8.2 %collective-permute-done.12 = bf16[64,2048]{1,0:T(8,128)(2,1)S(1)} collective-permute-done((bf16[64,2048]{1,0:T(8,128)(2,1)S(1)}, bf16[64,2048]{1,0:T(8,128)(2,1)S(1)}, u32[]{:S(2)}, u32[]{:S(2)}) %collective-permute-start.12) | collective-permute-done | bytes 262176 | tf_op jit(solution)/shard_map/ppermute | solution.py:22
  189.0 51.4 %all_to_all.5 = bf16[8,8,2048]{2,1,0:T(8,128)(2,1)S(1)} all-to-all(bf16[8,8,2048]{2,1,0:T(8,128)(2,1)S(1)} %fusion), channel_id=1, replica_groups={{0,32,64,96,128,160,192,224},{8,40,72,104,136,168,200,232},{16,48,80,11..., dimensions={0} | all-to-all | bytes 524288 | tf_op jit(solution)/shard_map/all_to_all | solution.py:44
  (24 shorter events, 6.6 us)
Async XLA Ops:
  0.0 36.7 %collective-permute-start.5 = (bf16[2,176,2048]{2,1,0:T(8,128)(2,1)}, bf16[2,176,2048]{2,1,0:T(8,128)(2,1)}, u32[]{:S(2)}, u32[]{:S(2)}) collective-permute-start(bf16[2,176,2048]{2,1,0:T(8,128)(2,1)} %bitcast.11), channel_id=1, source_target_pairs={{2,0},{0,2},{6,4},{4,6},{3,1},{1,3},{7,5},{5,7},{10,8},{8,10},{14,... | collective-permute-start | bytes 4325384 | tf_op jit(solution)/shard_map/ppermute | solution.py:57
  3.6 126.7 %collective-permute-start.8 = (bf16[176,2048]{1,0:T(8,128)(2,1)}, bf16[176,2048]{1,0:T(8,128)(2,1)}, u32[]{:S(2)}, u32[]{:S(2)}) collective-permute-start(bf16[176,2048]{1,0:T(8,128)(2,1)} %bitcast.15), channel_id=1, source_target_pairs={{2,0},{0,2},{6,4},{4,6},{3,1},{1,3},{7,5},{5,7},{10,8},{8,10},{14,... | collective-permute-start | bytes 2162696 | tf_op jit(solution)/shard_map/ppermute | solution.py:57
  5.9 148.4 %collective-permute-start.4 = (bf16[2,176,2048]{2,1,0:T(8,128)(2,1)}, bf16[2,176,2048]{2,1,0:T(8,128)(2,1)}, u32[]{:S(2)}, u32[]{:S(2)}) collective-permute-start(bf16[2,176,2048]{2,1,0:T(8,128)(2,1)} %bitcast.12), channel_id=1, source_target_pairs={{1,0},{0,1},{3,2},{2,3},{5,4},{4,5},{7,6},{6,7},{9,8},{8,9},{11,10... | collective-permute-start | bytes 4325384 | tf_op jit(solution)/shard_map/ppermute | solution.py:27
  36.7 117.6 %collective-permute-start.6 = (bf16[2,176,2048]{2,1,0:T(8,128)(2,1)}, bf16[2,176,2048]{2,1,0:T(8,128)(2,1)}, u32[]{:S(2)}, u32[]{:S(2)}) collective-permute-start(bf16[2,176,2048]{2,1,0:T(8,128)(2,1)} %collective-permute-done.5.refs_2_), channel_id=1, source_target_pairs={{1,0},{0,1},{3,2},{2,3},{5,4},{4,5},{7,6},{6,7},{9,8},{8,9},{11,10... | collective-permute-start | bytes 4325384 | tf_op jit(solution)/shard_map/ppermute | solution.py:27
  40.1 114.2 %copy-start.2 = (bf16[1,176,2048]{2,1,0:T(8,128)(2,1)S(1)}, bf16[1,176,2048]{2,1,0:T(8,128)(2,1)}, u32[]{:S(2)}) copy-start(bf16[1,176,2048]{2,1,0:T(8,128)(2,1)} %param.17) | copy-start | bytes 2162692
  113.7 14.6 %collective-permute-start = (bf16[64,2176]{1,0:T(8,128)(2,1)S(1)}, bf16[64,2176]{1,0:T(8,128)(2,1)S(1)}, u32[]{:S(2)}, u32[]{:S(2)}) collective-permute-start(bf16[64,2176]{1,0:T(8,128)(2,1)S(1)} %all_gather.3.refs_0_), channel_id=1, source_target_pairs={{8,0},{249,1},{16,8},{1,9},{24,16},{9,17},{32,24},{17,25},{40,32},... | collective-permute-start | bytes 835592 | tf_op jit(solution)/shard_map/ppermute | solution.py:22
  124.2 9.5 %collective-permute-start.1 = (bf16[64,2176]{1,0:T(8,128)(2,1)S(1)}, bf16[64,2176]{1,0:T(8,128)(2,1)S(1)}, u32[]{:S(2)}, u32[]{:S(2)}) collective-permute-start(bf16[64,2176]{1,0:T(8,128)(2,1)S(1)} %all_gather.3.refs_0_), channel_id=1, source_target_pairs={{16,0},{241,1},{24,8},{249,9},{32,16},{1,17},{40,24},{9,25},{48,32... | collective-permute-start | bytes 835592 | tf_op jit(solution)/shard_map/ppermute | solution.py:22
  128.3 26.0 %collective-permute-start.7 = (bf16[176,2048]{1,0:T(8,128)(2,1)}, bf16[176,2048]{1,0:T(8,128)(2,1)S(1)}, u32[]{:S(2)}, u32[]{:S(2)}) collective-permute-start(bf16[176,2048]{1,0:T(8,128)(2,1)} %bitcast.16), channel_id=1, source_target_pairs={{1,0},{0,1},{3,2},{2,3},{5,4},{4,5},{7,6},{6,7},{9,8},{8,9},{11,10... | collective-permute-start | bytes 2162696 | tf_op jit(solution)/shard_map/ppermute | solution.py:27
  130.3 24.0 %collective-permute-start.9 = (bf16[176,2048]{1,0:T(8,128)(2,1)}, bf16[176,2048]{1,0:T(8,128)(2,1)S(1)}, u32[]{:S(2)}, u32[]{:S(2)}) collective-permute-start(bf16[176,2048]{1,0:T(8,128)(2,1)} %collective-permute-done.8.refs_6_), channel_id=1, source_target_pairs={{1,0},{0,1},{3,2},{2,3},{5,4},{4,5},{7,6},{6,7},{9,8},{8,9},{11,10... | collective-permute-start | bytes 2162696 | tf_op jit(solution)/shard_map/ppermute | solution.py:27
  133.6 10.7 %collective-permute-start.2 = (bf16[64,2176]{1,0:T(8,128)(2,1)S(1)}, bf16[64,2176]{1,0:T(8,128)(2,1)S(1)}, u32[]{:S(2)}, u32[]{:S(2)}) collective-permute-start(bf16[64,2176]{1,0:T(8,128)(2,1)S(1)} %all_gather.3.refs_0_), channel_id=1, source_target_pairs={{248,0},{9,1},{0,8},{17,9},{8,16},{25,17},{16,24},{33,25},{24,32},... | collective-permute-start | bytes 835592 | tf_op jit(solution)/shard_map/ppermute | solution.py:22
  144.3 21.2 %copy-start.4 = (bf16[2048]{0:T(1024)(128)(2,1)S(1)}, bf16[2048]{0:T(1024)(128)(2,1)}, u32[]{:S(2)}) copy-start(bf16[2048]{0:T(1024)(128)(2,1)} %param.13) | copy-start | bytes 12292
  144.8 9.5 %collective-permute-start.3 = (bf16[64,2048]{1,0:T(8,128)(2,1)S(1)}, bf16[64,2048]{1,0:T(8,128)(2,1)S(1)}, u32[]{:S(2)}, u32[]{:S(2)}) collective-permute-start(bf16[64,2048]{1,0:T(8,128)(2,1)S(1)} %get-tuple-element.13.own_ref), channel_id=1, source_target_pairs={{6,0},{4,2},{2,4},{0,6},{7,1},{5,3},{3,5},{1,7},{14,8},{12,10},{10... | collective-permute-start | bytes 786440 | tf_op jit(solution)/shard_map/ppermute | solution.py:57
  154.3 1.4 copy-start
  155.7 9.8 %copy-start.1 = (bf16[2,2048,176]{1,2,0:T(8,128)(2,1)S(1)}, bf16[2,2048,176]{1,2,0:T(8,128)(2,1)}, u32[]{:S(2)}) copy-start(bf16[2,2048,176]{1,2,0:T(8,128)(2,1)} %param.14) | copy-start | bytes 4325380
  155.7 9.9 %copy-start.3 = (bf16[176,2048]{1,0:T(8,128)(2,1)S(1)}, bf16[176,2048]{1,0:T(8,128)(2,1)}, u32[]{:S(2)}) copy-start(bf16[176,2048]{1,0:T(8,128)(2,1)} %refs_6_.1) | copy-start | bytes 2162692
  160.4 9.5 %collective-permute-start.10 = (bf16[64,2048]{1,0:T(8,128)(2,1)S(1)}, bf16[64,2048]{1,0:T(8,128)(2,1)S(1)}, u32[]{:S(2)}, u32[]{:S(2)}) collective-permute-start(bf16[64,2048]{1,0:T(8,128)(2,1)S(1)} %get-tuple-element.15), channel_id=1, source_target_pairs={{6,0},{4,2},{2,4},{0,6},{7,1},{5,3},{3,5},{1,7},{14,8},{12,10},{10... | collective-permute-start | bytes 786440 | tf_op jit(solution)/shard_map/ppermute | solution.py:57
  170.3 10.3 %collective-permute-start.11 = (bf16[64,2048]{1,0:T(8,128)(2,1)S(1)}, bf16[64,2048]{1,0:T(8,128)(2,1)S(1)}, u32[]{:S(2)}, u32[]{:S(2)}) collective-permute-start(bf16[64,2048]{1,0:T(8,128)(2,1)S(1)} %get-tuple-element.18), channel_id=1, source_target_pairs={{248,0},{9,1},{0,8},{17,9},{8,16},{25,17},{16,24},{33,25},{24,32},... | collective-permute-start | bytes 786440 | tf_op jit(solution)/shard_map/ppermute | solution.py:22
  172.3 16.6 %collective-permute-start.12 = (bf16[64,2048]{1,0:T(8,128)(2,1)S(1)}, bf16[64,2048]{1,0:T(8,128)(2,1)S(1)}, u32[]{:S(2)}, u32[]{:S(2)}) collective-permute-start(bf16[64,2048]{1,0:T(8,128)(2,1)S(1)} %get-tuple-element.19), channel_id=1, source_target_pairs={{240,0},{17,1},{248,8},{25,9},{0,16},{33,17},{8,24},{41,25},{16,32... | collective-permute-start | bytes 786440 | tf_op jit(solution)/shard_map/ppermute | solution.py:22
  174.2 14.6 %collective-permute-start.13 = (bf16[64,2048]{1,0:T(8,128)(2,1)S(1)}, bf16[64,2048]{1,0:T(8,128)(2,1)S(1)}, u32[]{:S(2)}, u32[]{:S(2)}) collective-permute-start(bf16[64,2048]{1,0:T(8,128)(2,1)S(1)} %get-tuple-element.20), channel_id=1, source_target_pairs={{8,0},{249,1},{16,8},{1,9},{24,16},{9,17},{32,24},{17,25},{40,32},... | collective-permute-start | bytes 786440 | tf_op jit(solution)/shard_map/ppermute | solution.py:22

commit v2 on v1

--- a/solution.py
+++ b/solution.py
@@ -40,7 +40,8 @@
 def reduce_planes(own, sent, near, rows):
     total = own
     for block, k in zip(sent, (1, 2, -1)):
-        total = total + from_offset(block, "plane", -k).astype(jnp.float32)
+        arrived = from_offset(block, "plane", -k)
+        total = total + arrived.astype(jnp.float32)
     arrived = lax.all_to_all(
         total.astype(jnp.bfloat16).reshape(-1, rows, total.shape[1]),
         "plane",
@@ -69,22 +70,25 @@
     shards = (len(refs) - 5) // 2
     gate_up_refs, down_refs = refs[:shards], refs[shards : 2 * shards]
     kept_ref, sent_ref, gate_up, down, sems = refs[2 * shards :]
-    copies = []
-    for s in range(shards):
-        copies.append(pltpu.make_async_copy(gate_up_refs[s], gate_up.at[s], sems.at[2 * s]))
-        copies.append(pltpu.make_async_copy(down_refs[s], down.at[s], sems.at[2 * s + 1]))
-    for copy in copies:
-        copy.start()
+    fetch_in = pltpu.make_async_copy(gate_up_refs[-1], gate_up, sems.at[0])
+    fetch_out = pltpu.make_async_copy(down_refs[-1], down, sems.at[1])
+    fetch_in.start()
+    fetch_out.start()
     rows = jnp.concatenate([own_ref[...], other_ref[...]])
     contract = (((1,), (1,)), ((), ()))
     total = None
     for s in range(shards):
-        copies[2 * s].wait()
-        gate = lax.dot_general(rows, gate_up[s, 0], contract, preferred_element_type=jnp.float32)
-        up = lax.dot_general(rows, gate_up[s, 1], contract, preferred_element_type=jnp.float32)
+        last = s == shards - 1
+        if last:
+            fetch_in.wait()
+        both = gate_up if last else gate_up_refs[s]
+        gate = lax.dot_general(rows, both[0], contract, preferred_element_type=jnp.float32)
+        up = lax.dot_general(rows, both[1], contract, preferred_element_type=jnp.float32)
         hidden = (gate / (1.0 + jnp.exp(-gate)) * up).astype(jnp.bfloat16)
-        copies[2 * s + 1].wait()
-        part = jnp.dot(hidden, down[s], preferred_element_type=jnp.float32)
+        if last:
+            fetch_out.wait()
+        weights = down if last else down_refs[s]
+        part = jnp.dot(hidden, weights[...], preferred_element_type=jnp.float32)
         total = part if total is None else total + part
     half = own_ref.shape[0]
     kept_ref[...] = total[:half]
@@ -94,20 +98,21 @@
 def expert_partials(own, other, gate_ups, downs):
     rows, width = own.shape
     units = downs[0].shape[0]
-    vmem, anywhere = pl.BlockSpec(memory_space=pltpu.VMEM), pl.BlockSpec(memory_space=pl.ANY)
     shards = len(downs)
+    anywhere = pl.BlockSpec(memory_space=pl.ANY)
+    weights = in_vmem(shards - 1) + [anywhere]
     return pl.pallas_call(
         expert_kernel,
         out_shape=(
             jax.ShapeDtypeStruct((rows, width), jnp.float32),
             jax.ShapeDtypeStruct((rows, width), jnp.bfloat16),
         ),
-        in_specs=[vmem, vmem] + [anywhere] * (2 * shards),
-        out_specs=(vmem, vmem),
+        in_specs=in_vmem(2) + weights * 2,
+        out_specs=tuple(in_vmem(2)),
         scratch_shapes=[
-            pltpu.VMEM((shards, 2, units, width), jnp.bfloat16),
-            pltpu.VMEM((shards, units, width), jnp.bfloat16),
-            pltpu.SemaphoreType.DMA((2 * shards,)),
+            pltpu.VMEM((2, units, width), jnp.bfloat16),
+            pltpu.VMEM((units, width), jnp.bfloat16),
+            pltpu.SemaphoreType.DMA((2,)),
         ],
         compiler_params=pltpu.CompilerParams(vmem_limit_bytes=KERNEL_VMEM),
         cost_estimate=pl.CostEstimate(
@@ -268,8 +273,8 @@
     kept, sent = expert_partials(
         rows,
         other_rows,
-        (gate_up, gate_up_core, gate_up_chip, gate_up_far),
-        (down, down_core, down_chip, down_far),
+        (gate_up, gate_up_core, gate_up_far, gate_up_chip),
+        (down, down_core, down_far, down_chip),
     )
     got = from_chip(sent, row_partner)
 

time: 242 us -> 242 us (level)
  no operation moved by 1% of the time
where the time goes in v2:
time: 242 us; the launch traced here: 241 us
  blocking collectives  125 us (52%)
  waiting for transfers between devices  55.5 us (23%)
  starting transfers between devices  48.8 us (20%)
  Pallas kernels  9.51 us (4%)
    all_gather x1, blocking collectives, gather_planes(): own = lax.all_gather(block, 'plane', axis_index_groups=groups, tiled=True)  73.6 us
    all_to_all x1, blocking collectives, reduce_planes(): lax.all_to_all(total.astype(jnp.bfloat16).reshape(-1, rows, total.shape[1...  51.4 us
    ppermute x4, waiting for transfers between devices, from_chip(): lax.ppermute(block, 'depth', [(partner(i, size), i) for i in range(size)])  35.2 us
    ppermute x6, starting transfers between devices, from_offset(): return lax.ppermute(block, (axis, 'tok'), pairs)  24.4 us
    ppermute x6, waiting for transfers between devices, from_offset(): return lax.ppermute(block, (axis, 'tok'), pairs)  20.2 us
    ppermute x4, starting transfers between devices, from_chip(): lax.ppermute(block, 'depth', [(partner(i, size), i) for i in range(size)])  16.1 us
    ppermute x4, starting transfers between devices, from_core(): lax.ppermute(block, 'tok', [((i + 1) % size, i) for i in range(size)])  8.27 us
    pallas_call x1, Pallas kernels, expert_partials(): pl.pallas_call(expert_kernel, out_shape=(jax.ShapeDtypeStruct((rows, widt...  4.86 us
  transfers between devices with their start and end apart: 14, of which 8 were waited for; matrix products, arithmetic and copies ran while one was open for 0% of the time, Pallas kernels for 2%

profile of v2, /device:TPU:40, one launch (start us, length us, event | category | flops | bytes accessed | tf_op | source)
XLA Modules:
  0.0 241.2 jit_solution(4339833909754909124)
XLA Ops:
  0.0 3.6 %collective-permute-start.5 = (bf16[2,176,2048]{2,1,0:T(8,128)(2,1)}, bf16[2,176,2048]{2,1,0:T(8,128)(2,1)}, u32[]{:S(2)}, u32[]{:S(2)}) collective-permute-start(bf16[2,176,2048]{2,1,0:T(8,128)(2,1)} %bitcast.11), channel_id=1, source_target_pairs={{2,0},{0,2},{6,4},{4,6},{3,1},{1,3},{7,5},{5,7},{10,8},{8,10},{14,... | collective-permute-start | bytes 4325384 | tf_op jit(solution)/shard_map/ppermute | solution.py:58
  3.6 2.3 collective-permute-start.8
  5.9 2.0 collective-permute-start.4
  7.9 28.8 %collective-permute-done.5.refs_3_ = bf16[2,176,2048]{2,1,0:T(8,128)(2,1)} collective-permute-done((bf16[2,176,2048]{2,1,0:T(8,128)(2,1)}, bf16[2,176,2048]{2,1,0:T(8,128)(2,1)}, u32[]{:S(2)}, u32[]{:S(2)}) %collective-permute-start.5) | collective-permute-done | bytes 1441824 | tf_op jit(solution)/shard_map/ppermute | solution.py:58
  36.7 1.9 collective-permute-start.6
  40.1 73.6 %all_gather.3.refs_0_ = bf16[64,2176]{1,0:T(8,128)(2,1)S(1)} all-gather(bf16[8,2176]{1,0:T(8,128)(2,1)} %shard_map.91), channel_id=1, replica_groups={{0,32,64,96,128,160,192,224},{8,40,72,104,136,168,200,232},{16,48,80,11..., dimensions={0}, use_global_device_ids=true | all-gather | bytes 313344 | tf_op jit(solution)/shard_map/all_gather | solution.py:36
  113.7 10.4 %collective-permute-start = (bf16[64,2176]{1,0:T(8,128)(2,1)S(1)}, bf16[64,2176]{1,0:T(8,128)(2,1)S(1)}, u32[]{:S(2)}, u32[]{:S(2)}) collective-permute-start(bf16[64,2176]{1,0:T(8,128)(2,1)S(1)} %all_gather.3.refs_0_), channel_id=1, source_target_pairs={{8,0},{249,1},{16,8},{1,9},{24,16},{9,17},{32,24},{17,25},{40,32},... | collective-permute-start | bytes 835592 | tf_op jit(solution)/shard_map/ppermute | solution.py:22
  124.2 2.0 collective-permute-start.1
  126.1 2.2 collective-permute-done.refs_1_
  128.3 1.9 collective-permute-start.7
  130.3 2.4 %collective-permute-start.9 = (bf16[176,2048]{1,0:T(8,128)(2,1)}, bf16[176,2048]{1,0:T(8,128)(2,1)S(1)}, u32[]{:S(2)}, u32[]{:S(2)}) collective-permute-start(bf16[176,2048]{1,0:T(8,128)(2,1)} %collective-permute-done.8.refs_7_), channel_id=1, source_target_pairs={{1,0},{0,1},{3,2},{2,3},{5,4},{4,5},{7,6},{6,7},{9,8},{8,9},{11,10... | collective-permute-start | bytes 2162696 | tf_op jit(solution)/shard_map/ppermute | solution.py:27
  133.6 3.0 %collective-permute-start.2 = (bf16[64,2176]{1,0:T(8,128)(2,1)S(1)}, bf16[64,2176]{1,0:T(8,128)(2,1)S(1)}, u32[]{:S(2)}, u32[]{:S(2)}) collective-permute-start(bf16[64,2176]{1,0:T(8,128)(2,1)S(1)} %all_gather.3.refs_0_), channel_id=1, source_target_pairs={{248,0},{9,1},{0,8},{17,9},{8,16},{25,17},{16,24},{33,25},{24,32},... | collective-permute-start | bytes 835592 | tf_op jit(solution)/shard_map/ppermute | solution.py:22
  136.6 7.7 %collective-permute-done.2.refs_3_ = bf16[64,2176]{1,0:T(8,128)(2,1)S(1)} collective-permute-done((bf16[64,2176]{1,0:T(8,128)(2,1)S(1)}, bf16[64,2176]{1,0:T(8,128)(2,1)S(1)}, u32[]{:S(2)}, u32[]{:S(2)}) %collective-permute-start.2) | collective-permute-done | bytes 278560 | tf_op jit(solution)/shard_map/ppermute | solution.py:22
  144.8 5.1 %collective-permute-start.3 = (bf16[64,2048]{1,0:T(8,128)(2,1)S(1)}, bf16[64,2048]{1,0:T(8,128)(2,1)S(1)}, u32[]{:S(2)}, u32[]{:S(2)}) collective-permute-start(bf16[64,2048]{1,0:T(8,128)(2,1)S(1)} %get-tuple-element.13.own_ref), channel_id=1, source_target_pairs={{6,0},{4,2},{2,4},{0,6},{7,1},{5,3},{3,5},{1,7},{14,8},{12,10},{10... | collective-permute-start | bytes 786440 | tf_op jit(solution)/shard_map/ppermute | solution.py:58
  149.9 4.4 %collective-permute-done.3.other_ref = bf16[64,2048]{1,0:T(8,128)(2,1)S(1)} collective-permute-done((bf16[64,2048]{1,0:T(8,128)(2,1)S(1)}, bf16[64,2048]{1,0:T(8,128)(2,1)S(1)}, u32[]{:S(2)}, u32[]{:S(2)}) %collective-permute-start.3) | collective-permute-done | bytes 262176 | tf_op jit(solution)/shard_map/ppermute | solution.py:58
  155.7 4.9 %shard_map.93 = (f32[64,2048]{1,0:T(8,128)S(1)}, bf16[64,2048]{1,0:T(8,128)(2,1)S(1)}) custom-call(bf16[64,2048]{1,0:T(8,128)(2,1)S(1)} %get-tuple-element.13.own_ref, bf16[64,2048]{1,0:T(8,128)(2,1)S(1)} %collective-permute-done.3.other_ref, bf16[2,176,2048]{2,1,0:T(8,128)(2,1)S(1)} %bitcast.13, bf16[2,176,2048]{2,1,0:T(8,128)(2,1)} %collective-permute-done.4.refs_1_, ...), custom_call_target="tpu_custom_call" | custom-call | flops 1107296256 | bytes 8650752 | tf_op jit(solution)/shard_map/pallas_call | solution.py:104
  160.6 5.1 %collective-permute-start.10 = (bf16[64,2048]{1,0:T(8,128)(2,1)S(1)}, bf16[64,2048]{1,0:T(8,128)(2,1)S(1)}, u32[]{:S(2)}, u32[]{:S(2)}) collective-permute-start(bf16[64,2048]{1,0:T(8,128)(2,1)S(1)} %get-tuple-element.15), channel_id=1, source_target_pairs={{6,0},{4,2},{2,4},{0,6},{7,1},{5,3},{3,5},{1,7},{14,8},{12,10},{10... | collective-permute-start | bytes 786440 | tf_op jit(solution)/shard_map/ppermute | solution.py:58
  165.7 2.3 shard_map.94.shared_ref
  168.1 2.0 collective-permute-done.10.got_ref
  170.5 2.0 collective-permute-start.11
  172.4 2.0 collective-permute-start.12
  174.4 5.2 %collective-permute-start.13 = (bf16[64,2048]{1,0:T(8,128)(2,1)S(1)}, bf16[64,2048]{1,0:T(8,128)(2,1)S(1)}, u32[]{:S(2)}, u32[]{:S(2)}) collective-permute-start(bf16[64,2048]{1,0:T(8,128)(2,1)S(1)} %get-tuple-element.20), channel_id=1, source_target_pairs={{8,0},{249,1},{16,8},{1,9},{24,16},{9,17},{32,24},{17,25},{40,32},... | collective-permute-start | bytes 786440 | tf_op jit(solution)/shard_map/ppermute | solution.py:22
  180.8 8.2 %collective-permute-done.12 = bf16[64,2048]{1,0:T(8,128)(2,1)S(1)} collective-permute-done((bf16[64,2048]{1,0:T(8,128)(2,1)S(1)}, bf16[64,2048]{1,0:T(8,128)(2,1)S(1)}, u32[]{:S(2)}, u32[]{:S(2)}) %collective-permute-start.12) | collective-permute-done | bytes 262176 | tf_op jit(solution)/shard_map/ppermute | solution.py:22
  189.1 51.4 %all_to_all.5 = bf16[8,8,2048]{2,1,0:T(8,128)(2,1)S(1)} all-to-all(bf16[8,8,2048]{2,1,0:T(8,128)(2,1)S(1)} %fusion), channel_id=1, replica_groups={{0,32,64,96,128,160,192,224},{8,40,72,104,136,168,200,232},{16,48,80,11..., dimensions={0} | all-to-all | bytes 524288 | tf_op jit(solution)/shard_map/all_to_all | solution.py:45
  (24 shorter events, 6.6 us)
Async XLA Ops:
  0.0 36.7 %collective-permute-start.5 = (bf16[2,176,2048]{2,1,0:T(8,128)(2,1)}, bf16[2,176,2048]{2,1,0:T(8,128)(2,1)}, u32[]{:S(2)}, u32[]{:S(2)}) collective-permute-start(bf16[2,176,2048]{2,1,0:T(8,128)(2,1)} %bitcast.11), channel_id=1, source_target_pairs={{2,0},{0,2},{6,4},{4,6},{3,1},{1,3},{7,5},{5,7},{10,8},{8,10},{14,... | collective-permute-start | bytes 4325384 | tf_op jit(solution)/shard_map/ppermute | solution.py:58
  3.6 126.7 %collective-permute-start.8 = (bf16[176,2048]{1,0:T(8,128)(2,1)}, bf16[176,2048]{1,0:T(8,128)(2,1)}, u32[]{:S(2)}, u32[]{:S(2)}) collective-permute-start(bf16[176,2048]{1,0:T(8,128)(2,1)} %bitcast.15), channel_id=1, source_target_pairs={{2,0},{0,2},{6,4},{4,6},{3,1},{1,3},{7,5},{5,7},{10,8},{8,10},{14,... | collective-permute-start | bytes 2162696 | tf_op jit(solution)/shard_map/ppermute | solution.py:58
  5.9 148.4 %collective-permute-start.4 = (bf16[2,176,2048]{2,1,0:T(8,128)(2,1)}, bf16[2,176,2048]{2,1,0:T(8,128)(2,1)}, u32[]{:S(2)}, u32[]{:S(2)}) collective-permute-start(bf16[2,176,2048]{2,1,0:T(8,128)(2,1)} %bitcast.12), channel_id=1, source_target_pairs={{1,0},{0,1},{3,2},{2,3},{5,4},{4,5},{7,6},{6,7},{9,8},{8,9},{11,10... | collective-permute-start | bytes 4325384 | tf_op jit(solution)/shard_map/ppermute | solution.py:27
  36.7 117.6 %collective-permute-start.6 = (bf16[2,176,2048]{2,1,0:T(8,128)(2,1)}, bf16[2,176,2048]{2,1,0:T(8,128)(2,1)}, u32[]{:S(2)}, u32[]{:S(2)}) collective-permute-start(bf16[2,176,2048]{2,1,0:T(8,128)(2,1)} %collective-permute-done.5.refs_3_), channel_id=1, source_target_pairs={{1,0},{0,1},{3,2},{2,3},{5,4},{4,5},{7,6},{6,7},{9,8},{8,9},{11,10... | collective-permute-start | bytes 4325384 | tf_op jit(solution)/shard_map/ppermute | solution.py:27
  40.1 114.2 %copy-start.2 = (bf16[1,176,2048]{2,1,0:T(8,128)(2,1)S(1)}, bf16[1,176,2048]{2,1,0:T(8,128)(2,1)}, u32[]{:S(2)}) copy-start(bf16[1,176,2048]{2,1,0:T(8,128)(2,1)} %param.17) | copy-start | bytes 2162692
  113.7 14.6 %collective-permute-start = (bf16[64,2176]{1,0:T(8,128)(2,1)S(1)}, bf16[64,2176]{1,0:T(8,128)(2,1)S(1)}, u32[]{:S(2)}, u32[]{:S(2)}) collective-permute-start(bf16[64,2176]{1,0:T(8,128)(2,1)S(1)} %all_gather.3.refs_0_), channel_id=1, source_target_pairs={{8,0},{249,1},{16,8},{1,9},{24,16},{9,17},{32,24},{17,25},{40,32},... | collective-permute-start | bytes 835592 | tf_op jit(solution)/shard_map/ppermute | solution.py:22
  124.2 9.5 %collective-permute-start.1 = (bf16[64,2176]{1,0:T(8,128)(2,1)S(1)}, bf16[64,2176]{1,0:T(8,128)(2,1)S(1)}, u32[]{:S(2)}, u32[]{:S(2)}) collective-permute-start(bf16[64,2176]{1,0:T(8,128)(2,1)S(1)} %all_gather.3.refs_0_), channel_id=1, source_target_pairs={{16,0},{241,1},{24,8},{249,9},{32,16},{1,17},{40,24},{9,25},{48,32... | collective-permute-start | bytes 835592 | tf_op jit(solution)/shard_map/ppermute | solution.py:22
  128.3 26.0 %collective-permute-start.7 = (bf16[176,2048]{1,0:T(8,128)(2,1)}, bf16[176,2048]{1,0:T(8,128)(2,1)S(1)}, u32[]{:S(2)}, u32[]{:S(2)}) collective-permute-start(bf16[176,2048]{1,0:T(8,128)(2,1)} %bitcast.16), channel_id=1, source_target_pairs={{1,0},{0,1},{3,2},{2,3},{5,4},{4,5},{7,6},{6,7},{9,8},{8,9},{11,10... | collective-permute-start | bytes 2162696 | tf_op jit(solution)/shard_map/ppermute | solution.py:27
  130.3 24.0 %collective-permute-start.9 = (bf16[176,2048]{1,0:T(8,128)(2,1)}, bf16[176,2048]{1,0:T(8,128)(2,1)S(1)}, u32[]{:S(2)}, u32[]{:S(2)}) collective-permute-start(bf16[176,2048]{1,0:T(8,128)(2,1)} %collective-permute-done.8.refs_7_), channel_id=1, source_target_pairs={{1,0},{0,1},{3,2},{2,3},{5,4},{4,5},{7,6},{6,7},{9,8},{8,9},{11,10... | collective-permute-start | bytes 2162696 | tf_op jit(solution)/shard_map/ppermute | solution.py:27
  133.6 10.7 %collective-permute-start.2 = (bf16[64,2176]{1,0:T(8,128)(2,1)S(1)}, bf16[64,2176]{1,0:T(8,128)(2,1)S(1)}, u32[]{:S(2)}, u32[]{:S(2)}) collective-permute-start(bf16[64,2176]{1,0:T(8,128)(2,1)S(1)} %all_gather.3.refs_0_), channel_id=1, source_target_pairs={{248,0},{9,1},{0,8},{17,9},{8,16},{25,17},{16,24},{33,25},{24,32},... | collective-permute-start | bytes 835592 | tf_op jit(solution)/shard_map/ppermute | solution.py:22
  144.3 21.4 %copy-start.4 = (bf16[2048]{0:T(1024)(128)(2,1)S(1)}, bf16[2048]{0:T(1024)(128)(2,1)}, u32[]{:S(2)}) copy-start(bf16[2048]{0:T(1024)(128)(2,1)} %param.13) | copy-start | bytes 12292
  144.8 9.5 %collective-permute-start.3 = (bf16[64,2048]{1,0:T(8,128)(2,1)S(1)}, bf16[64,2048]{1,0:T(8,128)(2,1)S(1)}, u32[]{:S(2)}, u32[]{:S(2)}) collective-permute-start(bf16[64,2048]{1,0:T(8,128)(2,1)S(1)} %get-tuple-element.13.own_ref), channel_id=1, source_target_pairs={{6,0},{4,2},{2,4},{0,6},{7,1},{5,3},{3,5},{1,7},{14,8},{12,10},{10... | collective-permute-start | bytes 786440 | tf_op jit(solution)/shard_map/ppermute | solution.py:58
  154.3 1.4 copy-start
  155.7 10.0 %copy-start.1 = (bf16[2,2048,176]{1,2,0:T(8,128)(2,1)S(1)}, bf16[2,2048,176]{1,2,0:T(8,128)(2,1)}, u32[]{:S(2)}) copy-start(bf16[2,2048,176]{1,2,0:T(8,128)(2,1)} %param.14) | copy-start | bytes 4325380
  155.7 10.0 %copy-start.3 = (bf16[176,2048]{1,0:T(8,128)(2,1)S(1)}, bf16[176,2048]{1,0:T(8,128)(2,1)}, u32[]{:S(2)}) copy-start(bf16[176,2048]{1,0:T(8,128)(2,1)} %refs_6_.1) | copy-start | bytes 2162692
  160.6 9.5 %collective-permute-start.10 = (bf16[64,2048]{1,0:T(8,128)(2,1)S(1)}, bf16[64,2048]{1,0:T(8,128)(2,1)S(1)}, u32[]{:S(2)}, u32[]{:S(2)}) collective-permute-start(bf16[64,2048]{1,0:T(8,128)(2,1)S(1)} %get-tuple-element.15), channel_id=1, source_target_pairs={{6,0},{4,2},{2,4},{0,6},{7,1},{5,3},{3,5},{1,7},{14,8},{12,10},{10... | collective-permute-start | bytes 786440 | tf_op jit(solution)/shard_map/ppermute | solution.py:58
  170.5 10.3 %collective-permute-start.11 = (bf16[64,2048]{1,0:T(8,128)(2,1)S(1)}, bf16[64,2048]{1,0:T(8,128)(2,1)S(1)}, u32[]{:S(2)}, u32[]{:S(2)}) collective-permute-start(bf16[64,2048]{1,0:T(8,128)(2,1)S(1)} %get-tuple-element.18), channel_id=1, source_target_pairs={{248,0},{9,1},{0,8},{17,9},{8,16},{25,17},{16,24},{33,25},{24,32},... | collective-permute-start | bytes 786440 | tf_op jit(solution)/shard_map/ppermute | solution.py:22
  172.4 16.6 %collective-permute-start.12 = (bf16[64,2048]{1,0:T(8,128)(2,1)S(1)}, bf16[64,2048]{1,0:T(8,128)(2,1)S(1)}, u32[]{:S(2)}, u32[]{:S(2)}) collective-permute-start(bf16[64,2048]{1,0:T(8,128)(2,1)S(1)} %get-tuple-element.19), channel_id=1, source_target_pairs={{240,0},{17,1},{248,8},{25,9},{0,16},{33,17},{8,24},{41,25},{16,32... | collective-permute-start | bytes 786440 | tf_op jit(solution)/shard_map/ppermute | solution.py:22
  174.4 14.6 %collective-permute-start.13 = (bf16[64,2048]{1,0:T(8,128)(2,1)S(1)}, bf16[64,2048]{1,0:T(8,128)(2,1)S(1)}, u32[]{:S(2)}, u32[]{:S(2)}) collective-permute-start(bf16[64,2048]{1,0:T(8,128)(2,1)S(1)} %get-tuple-element.20), channel_id=1, source_target_pairs={{8,0},{249,1},{16,8},{1,9},{24,16},{9,17},{32,24},{17,25},{40,32},... | collective-permute-start | bytes 786440 | tf_op jit(solution)/shard_map/ppermute | solution.py:22

commit v3 on v2

--- a/solution.py
+++ b/solution.py
@@ -123,7 +123,7 @@
     )(own, other, *gate_ups, *downs)
 
 
-def notes_kernel(tokens_hbm, *refs, capacity):
+def notes_kernel(tokens_hbm, *refs):
     sources, out_ref, (ids_ref, slots_ref, weights_ref), sems = refs[:3], refs[3], refs[4:7], refs[7]
     width = tokens_hbm.shape[1]
     choices, rows = ids_ref.shape
@@ -134,14 +134,12 @@
         copy.start()
     for copy in copies[:3]:
         copy.wait()
-    slots = slots_ref[...]
-    code = jnp.where(slots < capacity, ids_ref[...] * capacity + slots, -1).astype(jnp.float32)
-    notes = jnp.concatenate([code, weights_ref[...].astype(jnp.float32)])
+    notes = jnp.concatenate([ref[...].astype(jnp.float32) for ref in targets])
     lane = lax.broadcasted_iota(jnp.int32, (rows, LANES), 1)
     row = lax.broadcasted_iota(jnp.int32, (rows, rows), 0)
     column = lax.broadcasted_iota(jnp.int32, (rows, rows), 1)
     placed = jnp.zeros((rows, LANES), jnp.float32)
-    for k in range(2 * choices):
+    for k in range(3 * choices):
         spread = jnp.where(row == column, notes[k : k + 1, :], 0.0)
         value = jnp.sum(spread, axis=1, keepdims=True)
         placed = jnp.where(lane == k, value, placed)
@@ -149,22 +147,26 @@
     copies[3].wait()
 
 
-def picks_kernel(first_ref, *refs, capacity, choices, tok_rows):
+def picks_kernel(expert_ref, *refs, capacity, choices, tok_rows):
     blocks, (rows_ref, mix_ref) = refs[:-2], refs[-2:]
     count, width = blocks[0].shape[0], rows_ref.shape[1]
     slots = mix_ref.shape[2]
     token = lax.broadcasted_iota(jnp.int32, (count, slots), 0)
     slot = lax.broadcasted_iota(jnp.int32, (count, slots), 1)
-    wanted = (first_ref[0] + slot % capacity).astype(jnp.float32)
+    mine = expert_ref[0].astype(jnp.float32)
+    wanted = (slot % capacity).astype(jnp.float32)
     here = slot // capacity == token // tok_rows
     for j, block in enumerate(blocks):
         notes = block[:, width:].astype(jnp.float32)
         weight = jnp.zeros((count, slots), jnp.float32)
         found = jnp.zeros((count, slots), jnp.float32)
         for k in range(choices):
-            match = here & (notes[:, k : k + 1] == wanted)
+            expert = notes[:, k : k + 1]
+            place = notes[:, choices + k : choices + k + 1]
+            value = notes[:, 2 * choices + k : 2 * choices + k + 1]
+            match = here & (expert == mine) & (place == wanted)
             found = jnp.where(match, 1.0, found)
-            weight = jnp.where(match, notes[:, choices + k : choices + k + 1], weight)
+            weight = jnp.where(match, value, weight)
         rows = lax.dot_general(
             found.astype(jnp.bfloat16),
             block[:, :width],
@@ -235,7 +237,7 @@
     small = pltpu.CompilerParams(vmem_limit_bytes=GLUE_VMEM)
 
     noted = pl.pallas_call(
-        functools.partial(notes_kernel, capacity=capacity),
+        notes_kernel,
         out_shape=jax.ShapeDtypeStruct((tok_rows, width + LANES), jnp.bfloat16),
         in_specs=[pl.BlockSpec(memory_space=pltpu.HBM)] * 4,
         out_specs=in_vmem(1)[0],
@@ -249,7 +251,7 @@
     )(tokens, expert_ids.T, slot_index.T, route_weight.T)
     blocks = gather_planes(noted, near)
 
-    first = (lax.axis_index("plane") * capacity).astype(jnp.int32).reshape(1)
+    expert = lax.axis_index("plane").astype(jnp.int32).reshape(1)
     rows, mix = pl.pallas_call(
         functools.partial(
             picks_kernel, capacity=capacity, choices=choices, tok_rows=tok_rows
@@ -261,7 +263,7 @@
         in_specs=[pl.BlockSpec(memory_space=pltpu.SMEM)] + in_vmem(near),
         out_specs=tuple(in_vmem(2)),
         compiler_params=small,
-    )(first, *blocks)
+    )(expert, *blocks)
 
     gate_up, down = expert_gate_up[0].swapaxes(1, 2), expert_down[0]
     gate_up_chip = from_chip(gate_up, weight_partner)

time: 242 us -> 242 us (level)
  no operation moved by 1% of the time
where the time goes in v3:
time: 242 us
  blocking collectives  125 us (52%)
  waiting for transfers between devices  55.5 us (23%)
  starting transfers between devices  48.8 us (20%)
  Pallas kernels  9.87 us (4%)
    all_gather x1, blocking collectives, gather_planes(): own = lax.all_gather(block, 'plane', axis_index_groups=groups, tiled=True)  73.6 us
    all_to_all x1, blocking collectives, reduce_planes(): lax.all_to_all(total.astype(jnp.bfloat16).reshape(-1, rows, total.shape[1...  51.4 us
    ppermute x4, waiting for transfers between devices, from_chip(): lax.ppermute(block, 'depth', [(partner(i, size), i) for i in range(size)])  35.2 us
    ppermute x6, starting transfers between devices, from_offset(): return lax.ppermute(block, (axis, 'tok'), pairs)  24.4 us
    ppermute x6, waiting for transfers between devices, from_offset(): return lax.ppermute(block, (axis, 'tok'), pairs)  20.2 us
    ppermute x4, starting transfers between devices, from_chip(): lax.ppermute(block, 'depth', [(partner(i, size), i) for i in range(size)])  16.1 us
    ppermute x4, starting transfers between devices, from_core(): lax.ppermute(block, 'tok', [((i + 1) % size, i) for i in range(size)])  8.27 us
    pallas_call x1, Pallas kernels, expert_partials(): pl.pallas_call(expert_kernel, out_shape=(jax.ShapeDtypeStruct((rows, widt...  4.85 us
  transfers between devices with their start and end apart: 14, of which 8 were waited for; matrix products, arithmetic and copies ran while one was open for 0% of the time, Pallas kernels for 2%

profile of v3, /device:TPU:40, one launch (start us, length us, event | category | flops | bytes accessed | tf_op | source)
XLA Modules:
  0.0 241.6 jit_solution(15475493346127803589)
XLA Ops:
  0.0 3.6 %collective-permute-start.5 = (bf16[2,176,2048]{2,1,0:T(8,128)(2,1)}, bf16[2,176,2048]{2,1,0:T(8,128)(2,1)}, u32[]{:S(2)}, u32[]{:S(2)}) collective-permute-start(bf16[2,176,2048]{2,1,0:T(8,128)(2,1)} %bitcast.11), channel_id=1, source_target_pairs={{2,0},{0,2},{6,4},{4,6},{3,1},{1,3},{7,5},{5,7},{10,8},{8,10},{14,... | collective-permute-start | bytes 4325384 | tf_op jit(solution)/shard_map/ppermute | solution.py:58
  3.6 2.3 collective-permute-start.8
  5.9 2.0 collective-permute-start.4
  7.9 28.8 %collective-permute-done.5.refs_3_ = bf16[2,176,2048]{2,1,0:T(8,128)(2,1)} collective-permute-done((bf16[2,176,2048]{2,1,0:T(8,128)(2,1)}, bf16[2,176,2048]{2,1,0:T(8,128)(2,1)}, u32[]{:S(2)}, u32[]{:S(2)}) %collective-permute-start.5) | collective-permute-done | bytes 1441824 | tf_op jit(solution)/shard_map/ppermute | solution.py:58
  36.7 1.9 collective-permute-start.6
  40.1 73.6 %all_gather.3.refs_0_ = bf16[64,2176]{1,0:T(8,128)(2,1)S(1)} all-gather(bf16[8,2176]{1,0:T(8,128)(2,1)} %shard_map.91), channel_id=1, replica_groups={{0,32,64,96,128,160,192,224},{8,40,72,104,136,168,200,232},{16,48,80,11..., dimensions={0}, use_global_device_ids=true | all-gather | bytes 313344 | tf_op jit(solution)/shard_map/all_gather | solution.py:36
  113.7 10.4 %collective-permute-start = (bf16[64,2176]{1,0:T(8,128)(2,1)S(1)}, bf16[64,2176]{1,0:T(8,128)(2,1)S(1)}, u32[]{:S(2)}, u32[]{:S(2)}) collective-permute-start(bf16[64,2176]{1,0:T(8,128)(2,1)S(1)} %all_gather.3.refs_0_), channel_id=1, source_target_pairs={{8,0},{249,1},{16,8},{1,9},{24,16},{9,17},{32,24},{17,25},{40,32},... | collective-permute-start | bytes 835592 | tf_op jit(solution)/shard_map/ppermute | solution.py:22
  124.2 2.0 collective-permute-start.1
  126.1 2.2 collective-permute-done.refs_1_
  128.3 1.9 collective-permute-start.7
  130.3 2.4 %collective-permute-start.9 = (bf16[176,2048]{1,0:T(8,128)(2,1)}, bf16[176,2048]{1,0:T(8,128)(2,1)S(1)}, u32[]{:S(2)}, u32[]{:S(2)}) collective-permute-start(bf16[176,2048]{1,0:T(8,128)(2,1)} %collective-permute-done.8.refs_7_), channel_id=1, source_target_pairs={{1,0},{0,1},{3,2},{2,3},{5,4},{4,5},{7,6},{6,7},{9,8},{8,9},{11,10... | collective-permute-start | bytes 2162696 | tf_op jit(solution)/shard_map/ppermute | solution.py:27
  133.6 3.0 %collective-permute-start.2 = (bf16[64,2176]{1,0:T(8,128)(2,1)S(1)}, bf16[64,2176]{1,0:T(8,128)(2,1)S(1)}, u32[]{:S(2)}, u32[]{:S(2)}) collective-permute-start(bf16[64,2176]{1,0:T(8,128)(2,1)S(1)} %all_gather.3.refs_0_), channel_id=1, source_target_pairs={{248,0},{9,1},{0,8},{17,9},{8,16},{25,17},{16,24},{33,25},{24,32},... | collective-permute-start | bytes 835592 | tf_op jit(solution)/shard_map/ppermute | solution.py:22
  136.6 7.7 %collective-permute-done.2.refs_3_ = bf16[64,2176]{1,0:T(8,128)(2,1)S(1)} collective-permute-done((bf16[64,2176]{1,0:T(8,128)(2,1)S(1)}, bf16[64,2176]{1,0:T(8,128)(2,1)S(1)}, u32[]{:S(2)}, u32[]{:S(2)}) %collective-permute-start.2) | collective-permute-done | bytes 278560 | tf_op jit(solution)/shard_map/ppermute | solution.py:22
  145.2 5.1 %collective-permute-start.3 = (bf16[64,2048]{1,0:T(8,128)(2,1)S(1)}, bf16[64,2048]{1,0:T(8,128)(2,1)S(1)}, u32[]{:S(2)}, u32[]{:S(2)}) collective-permute-start(bf16[64,2048]{1,0:T(8,128)(2,1)S(1)} %get-tuple-element.13.own_ref), channel_id=1, source_target_pairs={{6,0},{4,2},{2,4},{0,6},{7,1},{5,3},{3,5},{1,7},{14,8},{12,10},{10... | collective-permute-start | bytes 786440 | tf_op jit(solution)/shard_map/ppermute | solution.py:58
  150.3 4.4 %collective-permute-done.3.other_ref = bf16[64,2048]{1,0:T(8,128)(2,1)S(1)} collective-permute-done((bf16[64,2048]{1,0:T(8,128)(2,1)S(1)}, bf16[64,2048]{1,0:T(8,128)(2,1)S(1)}, u32[]{:S(2)}, u32[]{:S(2)}) %collective-permute-start.3) | collective-permute-done | bytes 262176 | tf_op jit(solution)/shard_map/ppermute | solution.py:58
  156.1 4.8 %shard_map.93 = (f32[64,2048]{1,0:T(8,128)S(1)}, bf16[64,2048]{1,0:T(8,128)(2,1)S(1)}) custom-call(bf16[64,2048]{1,0:T(8,128)(2,1)S(1)} %get-tuple-element.13.own_ref, bf16[64,2048]{1,0:T(8,128)(2,1)S(1)} %collective-permute-done.3.other_ref, bf16[2,176,2048]{2,1,0:T(8,128)(2,1)S(1)} %bitcast.13, bf16[2,176,2048]{2,1,0:T(8,128)(2,1)} %collective-permute-done.4.refs_1_, ...), custom_call_target="tpu_custom_call" | custom-call | flops 1107296256 | bytes 8650752 | tf_op jit(solution)/shard_map/pallas_call | solution.py:104
  160.9 5.1 %collective-permute-start.10 = (bf16[64,2048]{1,0:T(8,128)(2,1)S(1)}, bf16[64,2048]{1,0:T(8,128)(2,1)S(1)}, u32[]{:S(2)}, u32[]{:S(2)}) collective-permute-start(bf16[64,2048]{1,0:T(8,128)(2,1)S(1)} %get-tuple-element.15), channel_id=1, source_target_pairs={{6,0},{4,2},{2,4},{0,6},{7,1},{5,3},{3,5},{1,7},{14,8},{12,10},{10... | collective-permute-start | bytes 786440 | tf_op jit(solution)/shard_map/ppermute | solution.py:58
  166.1 2.3 shard_map.94.shared_ref
  168.4 2.0 collective-permute-done.10.got_ref
  170.8 2.0 collective-permute-start.11
  172.8 2.0 collective-permute-start.12
  174.8 5.2 %collective-permute-start.13 = (bf16[64,2048]{1,0:T(8,128)(2,1)S(1)}, bf16[64,2048]{1,0:T(8,128)(2,1)S(1)}, u32[]{:S(2)}, u32[]{:S(2)}) collective-permute-start(bf16[64,2048]{1,0:T(8,128)(2,1)S(1)} %get-tuple-element.20), channel_id=1, source_target_pairs={{8,0},{249,1},{16,8},{1,9},{24,16},{9,17},{32,24},{17,25},{40,32},... | collective-permute-start | bytes 786440 | tf_op jit(solution)/shard_map/ppermute | solution.py:22
  181.1 8.2 %collective-permute-done.12 = bf16[64,2048]{1,0:T(8,128)(2,1)S(1)} collective-permute-done((bf16[64,2048]{1,0:T(8,128)(2,1)S(1)}, bf16[64,2048]{1,0:T(8,128)(2,1)S(1)}, u32[]{:S(2)}, u32[]{:S(2)}) %collective-permute-start.12) | collective-permute-done | bytes 262176 | tf_op jit(solution)/shard_map/ppermute | solution.py:22
  189.5 51.4 %all_to_all.5 = bf16[8,8,2048]{2,1,0:T(8,128)(2,1)S(1)} all-to-all(bf16[8,8,2048]{2,1,0:T(8,128)(2,1)S(1)} %fusion), channel_id=1, replica_groups={{0,32,64,96,128,160,192,224},{8,40,72,104,136,168,200,232},{16,48,80,11..., dimensions={0} | all-to-all | bytes 524288 | tf_op jit(solution)/shard_map/all_to_all | solution.py:45
  (24 shorter events, 7.0 us)
Async XLA Ops:
  0.0 36.7 %collective-permute-start.5 = (bf16[2,176,2048]{2,1,0:T(8,128)(2,1)}, bf16[2,176,2048]{2,1,0:T(8,128)(2,1)}, u32[]{:S(2)}, u32[]{:S(2)}) collective-permute-start(bf16[2,176,2048]{2,1,0:T(8,128)(2,1)} %bitcast.11), channel_id=1, source_target_pairs={{2,0},{0,2},{6,4},{4,6},{3,1},{1,3},{7,5},{5,7},{10,8},{8,10},{14,... | collective-permute-start | bytes 4325384 | tf_op jit(solution)/shard_map/ppermute | solution.py:58
  3.6 126.7 %collective-permute-start.8 = (bf16[176,2048]{1,0:T(8,128)(2,1)}, bf16[176,2048]{1,0:T(8,128)(2,1)}, u32[]{:S(2)}, u32[]{:S(2)}) collective-permute-start(bf16[176,2048]{1,0:T(8,128)(2,1)} %bitcast.15), channel_id=1, source_target_pairs={{2,0},{0,2},{6,4},{4,6},{3,1},{1,3},{7,5},{5,7},{10,8},{8,10},{14,... | collective-permute-start | bytes 2162696 | tf_op jit(solution)/shard_map/ppermute | solution.py:58
  5.9 148.8 %collective-permute-start.4 = (bf16[2,176,2048]{2,1,0:T(8,128)(2,1)}, bf16[2,176,2048]{2,1,0:T(8,128)(2,1)}, u32[]{:S(2)}, u32[]{:S(2)}) collective-permute-start(bf16[2,176,2048]{2,1,0:T(8,128)(2,1)} %bitcast.12), channel_id=1, source_target_pairs={{1,0},{0,1},{3,2},{2,3},{5,4},{4,5},{7,6},{6,7},{9,8},{8,9},{11,10... | collective-permute-start | bytes 4325384 | tf_op jit(solution)/shard_map/ppermute | solution.py:27
  36.7 118.0 %collective-permute-start.6 = (bf16[2,176,2048]{2,1,0:T(8,128)(2,1)}, bf16[2,176,2048]{2,1,0:T(8,128)(2,1)}, u32[]{:S(2)}, u32[]{:S(2)}) collective-permute-start(bf16[2,176,2048]{2,1,0:T(8,128)(2,1)} %collective-permute-done.5.refs_3_), channel_id=1, source_target_pairs={{1,0},{0,1},{3,2},{2,3},{5,4},{4,5},{7,6},{6,7},{9,8},{8,9},{11,10... | collective-permute-start | bytes 4325384 | tf_op jit(solution)/shard_map/ppermute | solution.py:27
  40.1 114.6 %copy-start.2 = (bf16[1,176,2048]{2,1,0:T(8,128)(2,1)S(1)}, bf16[1,176,2048]{2,1,0:T(8,128)(2,1)}, u32[]{:S(2)}) copy-start(bf16[1,176,2048]{2,1,0:T(8,128)(2,1)} %param.17) | copy-start | bytes 2162692
  113.7 14.6 %collective-permute-start = (bf16[64,2176]{1,0:T(8,128)(2,1)S(1)}, bf16[64,2176]{1,0:T(8,128)(2,1)S(1)}, u32[]{:S(2)}, u32[]{:S(2)}) collective-permute-start(bf16[64,2176]{1,0:T(8,128)(2,1)S(1)} %all_gather.3.refs_0_), channel_id=1, source_target_pairs={{8,0},{249,1},{16,8},{1,9},{24,16},{9,17},{32,24},{17,25},{40,32},... | collective-permute-start | bytes 835592 | tf_op jit(solution)/shard_map/ppermute | solution.py:22
  124.2 9.5 %collective-permute-start.1 = (bf16[64,2176]{1,0:T(8,128)(2,1)S(1)}, bf16[64,2176]{1,0:T(8,128)(2,1)S(1)}, u32[]{:S(2)}, u32[]{:S(2)}) collective-permute-start(bf16[64,2176]{1,0:T(8,128)(2,1)S(1)} %all_gather.3.refs_0_), channel_id=1, source_target_pairs={{16,0},{241,1},{24,8},{249,9},{32,16},{1,17},{40,24},{9,25},{48,32... | collective-permute-start | bytes 835592 | tf_op jit(solution)/shard_map/ppermute | solution.py:22
  128.3 26.3 %collective-permute-start.7 = (bf16[176,2048]{1,0:T(8,128)(2,1)}, bf16[176,2048]{1,0:T(8,128)(2,1)S(1)}, u32[]{:S(2)}, u32[]{:S(2)}) collective-permute-start(bf16[176,2048]{1,0:T(8,128)(2,1)} %bitcast.16), channel_id=1, source_target_pairs={{1,0},{0,1},{3,2},{2,3},{5,4},{4,5},{7,6},{6,7},{9,8},{8,9},{11,10... | collective-permute-start | bytes 2162696 | tf_op jit(solution)/shard_map/ppermute | solution.py:27
  130.3 24.4 %collective-permute-start.9 = (bf16[176,2048]{1,0:T(8,128)(2,1)}, bf16[176,2048]{1,0:T(8,128)(2,1)S(1)}, u32[]{:S(2)}, u32[]{:S(2)}) collective-permute-start(bf16[176,2048]{1,0:T(8,128)(2,1)} %collective-permute-done.8.refs_7_), channel_id=1, source_target_pairs={{1,0},{0,1},{3,2},{2,3},{5,4},{4,5},{7,6},{6,7},{9,8},{8,9},{11,10... | collective-permute-start | bytes 2162696 | tf_op jit(solution)/shard_map/ppermute | solution.py:27
  133.6 10.7 %collective-permute-start.2 = (bf16[64,2176]{1,0:T(8,128)(2,1)S(1)}, bf16[64,2176]{1,0:T(8,128)(2,1)S(1)}, u32[]{:S(2)}, u32[]{:S(2)}) collective-permute-start(bf16[64,2176]{1,0:T(8,128)(2,1)S(1)} %all_gather.3.refs_0_), channel_id=1, source_target_pairs={{248,0},{9,1},{0,8},{17,9},{8,16},{25,17},{16,24},{33,25},{24,32},... | collective-permute-start | bytes 835592 | tf_op jit(solution)/shard_map/ppermute | solution.py:22
  144.3 21.7 %copy-start.4 = (bf16[2048]{0:T(1024)(128)(2,1)S(1)}, bf16[2048]{0:T(1024)(128)(2,1)}, u32[]{:S(2)}) copy-start(bf16[2048]{0:T(1024)(128)(2,1)} %param.13) | copy-start | bytes 12292
  145.2 9.5 %collective-permute-start.3 = (bf16[64,2048]{1,0:T(8,128)(2,1)S(1)}, bf16[64,2048]{1,0:T(8,128)(2,1)S(1)}, u32[]{:S(2)}, u32[]{:S(2)}) collective-permute-start(bf16[64,2048]{1,0:T(8,128)(2,1)S(1)} %get-tuple-element.13.own_ref), channel_id=1, source_target_pairs={{6,0},{4,2},{2,4},{0,6},{7,1},{5,3},{3,5},{1,7},{14,8},{12,10},{10... | collective-permute-start | bytes 786440 | tf_op jit(solution)/shard_map/ppermute | solution.py:58
  154.7 1.4 copy-start
  156.1 10.0 %copy-start.1 = (bf16[2,2048,176]{1,2,0:T(8,128)(2,1)S(1)}, bf16[2,2048,176]{1,2,0:T(8,128)(2,1)}, u32[]{:S(2)}) copy-start(bf16[2,2048,176]{1,2,0:T(8,128)(2,1)} %param.14) | copy-start | bytes 4325380
  156.1 10.0 %copy-start.3 = (bf16[176,2048]{1,0:T(8,128)(2,1)S(1)}, bf16[176,2048]{1,0:T(8,128)(2,1)}, u32[]{:S(2)}) copy-start(bf16[176,2048]{1,0:T(8,128)(2,1)} %refs_6_.1) | copy-start | bytes 2162692
  160.9 9.5 %collective-permute-start.10 = (bf16[64,2048]{1,0:T(8,128)(2,1)S(1)}, bf16[64,2048]{1,0:T(8,128)(2,1)S(1)}, u32[]{:S(2)}, u32[]{:S(2)}) collective-permute-start(bf16[64,2048]{1,0:T(8,128)(2,1)S(1)} %get-tuple-element.15), channel_id=1, source_target_pairs={{6,0},{4,2},{2,4},{0,6},{7,1},{5,3},{3,5},{1,7},{14,8},{12,10},{10... | collective-permute-start | bytes 786440 | tf_op jit(solution)/shard_map/ppermute | solution.py:58
  170.8 10.3 %collective-permute-start.11 = (bf16[64,2048]{1,0:T(8,128)(2,1)S(1)}, bf16[64,2048]{1,0:T(8,128)(2,1)S(1)}, u32[]{:S(2)}, u32[]{:S(2)}) collective-permute-start(bf16[64,2048]{1,0:T(8,128)(2,1)S(1)} %get-tuple-element.18), channel_id=1, source_target_pairs={{248,0},{9,1},{0,8},{17,9},{8,16},{25,17},{16,24},{33,25},{24,32},... | collective-permute-start | bytes 786440 | tf_op jit(solution)/shard_map/ppermute | solution.py:22
  172.8 16.6 %collective-permute-start.12 = (bf16[64,2048]{1,0:T(8,128)(2,1)S(1)}, bf16[64,2048]{1,0:T(8,128)(2,1)S(1)}, u32[]{:S(2)}, u32[]{:S(2)}) collective-permute-start(bf16[64,2048]{1,0:T(8,128)(2,1)S(1)} %get-tuple-element.19), channel_id=1, source_target_pairs={{240,0},{17,1},{248,8},{25,9},{0,16},{33,17},{8,24},{41,25},{16,32... | collective-permute-start | bytes 786440 | tf_op jit(solution)/shard_map/ppermute | solution.py:22
  174.8 14.6 %collective-permute-start.13 = (bf16[64,2048]{1,0:T(8,128)(2,1)S(1)}, bf16[64,2048]{1,0:T(8,128)(2,1)S(1)}, u32[]{:S(2)}, u32[]{:S(2)}) collective-permute-start(bf16[64,2048]{1,0:T(8,128)(2,1)S(1)} %get-tuple-element.20), channel_id=1, source_target_pairs={{8,0},{249,1},{16,8},{1,9},{24,16},{9,17},{32,24},{17,25},{40,32},... | collective-permute-start | bytes 786440 | tf_op jit(solution)/shard_map/ppermute | solution.py:22

commit v4 on v3

--- a/solution.py
+++ b/solution.py
@@ -126,7 +126,7 @@
 def notes_kernel(tokens_hbm, *refs):
     sources, out_ref, (ids_ref, slots_ref, weights_ref), sems = refs[:3], refs[3], refs[4:7], refs[7]
     width = tokens_hbm.shape[1]
-    choices, rows = ids_ref.shape
+    choices = ids_ref.shape[0]
     targets = (ids_ref, slots_ref, weights_ref)
     copies = [pltpu.make_async_copy(a, b, sems.at[i]) for i, (a, b) in enumerate(zip(sources, targets))]
     copies.append(pltpu.make_async_copy(tokens_hbm, out_ref.at[:, pl.ds(0, width)], sems.at[3]))
@@ -135,14 +135,14 @@
     for copy in copies[:3]:
         copy.wait()
     notes = jnp.concatenate([ref[...].astype(jnp.float32) for ref in targets])
-    lane = lax.broadcasted_iota(jnp.int32, (rows, LANES), 1)
-    row = lax.broadcasted_iota(jnp.int32, (rows, rows), 0)
-    column = lax.broadcasted_iota(jnp.int32, (rows, rows), 1)
-    placed = jnp.zeros((rows, LANES), jnp.float32)
-    for k in range(3 * choices):
-        spread = jnp.where(row == column, notes[k : k + 1, :], 0.0)
-        value = jnp.sum(spread, axis=1, keepdims=True)
-        placed = jnp.where(lane == k, value, placed)
+    kind = lax.broadcasted_iota(jnp.int32, (3 * choices, LANES), 0)
+    lane = lax.broadcasted_iota(jnp.int32, (3 * choices, LANES), 1)
+    placed = lax.dot_general(
+        notes.astype(jnp.bfloat16),
+        jnp.where(kind == lane, 1.0, 0.0).astype(jnp.bfloat16),
+        (((0,), (0,)), ((), ())),
+        preferred_element_type=jnp.float32,
+    )
     out_ref[:, width:] = placed.astype(jnp.bfloat16)
     copies[3].wait()
 
@@ -153,18 +153,17 @@
     slots = mix_ref.shape[2]
     token = lax.broadcasted_iota(jnp.int32, (count, slots), 0)
     slot = lax.broadcasted_iota(jnp.int32, (count, slots), 1)
-    mine = expert_ref[0].astype(jnp.float32)
-    wanted = (slot % capacity).astype(jnp.float32)
+    wanted = (expert_ref[0] * capacity + slot % capacity).astype(jnp.float32)
     here = slot // capacity == token // tok_rows
     for j, block in enumerate(blocks):
         notes = block[:, width:].astype(jnp.float32)
+        experts, places = notes[:, :choices], notes[:, choices : 2 * choices]
+        code = jnp.where(places < capacity, experts * capacity + places, -1.0)
         weight = jnp.zeros((count, slots), jnp.float32)
         found = jnp.zeros((count, slots), jnp.float32)
         for k in range(choices):
-            expert = notes[:, k : k + 1]
-            place = notes[:, choices + k : choices + k + 1]
             value = notes[:, 2 * choices + k : 2 * choices + k + 1]
-            match = here & (expert == mine) & (place == wanted)
+            match = here & (code[:, k : k + 1] == wanted)
             found = jnp.where(match, 1.0, found)
             weight = jnp.where(match, value, weight)
         rows = lax.dot_general(

time: 242 us -> 242 us (level)
  no operation moved by 1% of the time
where the time goes in v4:
time: 242 us
  blocking collectives  125 us (52%)
  waiting for transfers between devices  55.5 us (23%)
  starting transfers between devices  48.8 us (20%)
  Pallas kernels  10 us (4%)
    all_gather x1, blocking collectives, gather_planes(): own = lax.all_gather(block, 'plane', axis_index_groups=groups, tiled=True)  73.6 us
    all_to_all x1, blocking collectives, reduce_planes(): lax.all_to_all(total.astype(jnp.bfloat16).reshape(-1, rows, total.shape[1...  51.4 us
    ppermute x4, waiting for transfers between devices, from_chip(): lax.ppermute(block, 'depth', [(partner(i, size), i) for i in range(size)])  35.2 us
    ppermute x6, starting transfers between devices, from_offset(): return lax.ppermute(block, (axis, 'tok'), pairs)  24.4 us
    ppermute x6, waiting for transfers between devices, from_offset(): return lax.ppermute(block, (axis, 'tok'), pairs)  20.2 us
    ppermute x4, starting transfers between devices, from_chip(): lax.ppermute(block, 'depth', [(partner(i, size), i) for i in range(size)])  16.1 us
    ppermute x4, starting transfers between devices, from_core(): lax.ppermute(block, 'tok', [((i + 1) % size, i) for i in range(size)])  8.27 us
    pallas_call x1, Pallas kernels, expert_partials(): pl.pallas_call(expert_kernel, out_shape=(jax.ShapeDtypeStruct((rows, widt...  4.85 us
  transfers between devices with their start and end apart: 14, of which 8 were waited for; matrix products, arithmetic and copies ran while one was open for 0% of the time, Pallas kernels for 2%

profile of v4, /device:TPU:40, one launch (start us, length us, event | category | flops | bytes accessed | tf_op | source)
XLA Modules:
  0.0 241.7 jit_solution(794310356761012713)
XLA Ops:
  0.0 3.6 %collective-permute-start.5 = (bf16[2,176,2048]{2,1,0:T(8,128)(2,1)}, bf16[2,176,2048]{2,1,0:T(8,128)(2,1)}, u32[]{:S(2)}, u32[]{:S(2)}) collective-permute-start(bf16[2,176,2048]{2,1,0:T(8,128)(2,1)} %bitcast.11), channel_id=1, source_target_pairs={{2,0},{0,2},{6,4},{4,6},{3,1},{1,3},{7,5},{5,7},{10,8},{8,10},{14,... | collective-permute-start | bytes 4325384 | tf_op jit(solution)/shard_map/ppermute | solution.py:58
  3.6 2.3 collective-permute-start.8
  5.9 2.0 collective-permute-start.4
  7.9 28.8 %collective-permute-done.5.refs_3_ = bf16[2,176,2048]{2,1,0:T(8,128)(2,1)} collective-permute-done((bf16[2,176,2048]{2,1,0:T(8,128)(2,1)}, bf16[2,176,2048]{2,1,0:T(8,128)(2,1)}, u32[]{:S(2)}, u32[]{:S(2)}) %collective-permute-start.5) | collective-permute-done | bytes 1441824 | tf_op jit(solution)/shard_map/ppermute | solution.py:58
  36.7 1.9 collective-permute-start.6
  40.2 73.6 %all_gather.3.refs_0_ = bf16[64,2176]{1,0:T(8,128)(2,1)S(1)} all-gather(bf16[8,2176]{1,0:T(8,128)(2,1)} %shard_map.91), channel_id=1, replica_groups={{0,32,64,96,128,160,192,224},{8,40,72,104,136,168,200,232},{16,48,80,11..., dimensions={0}, use_global_device_ids=true | all-gather | bytes 313344 | tf_op jit(solution)/shard_map/all_gather | solution.py:36
  113.8 10.4 %collective-permute-start = (bf16[64,2176]{1,0:T(8,128)(2,1)S(1)}, bf16[64,2176]{1,0:T(8,128)(2,1)S(1)}, u32[]{:S(2)}, u32[]{:S(2)}) collective-permute-start(bf16[64,2176]{1,0:T(8,128)(2,1)S(1)} %all_gather.3.refs_0_), channel_id=1, source_target_pairs={{8,0},{249,1},{16,8},{1,9},{24,16},{9,17},{32,24},{17,25},{40,32},... | collective-permute-start | bytes 835592 | tf_op jit(solution)/shard_map/ppermute | solution.py:22
  124.2 2.0 collective-permute-start.1
  126.2 2.2 collective-permute-done.refs_1_
  128.4 1.9 collective-permute-start.7
  130.4 2.4 %collective-permute-start.9 = (bf16[176,2048]{1,0:T(8,128)(2,1)}, bf16[176,2048]{1,0:T(8,128)(2,1)S(1)}, u32[]{:S(2)}, u32[]{:S(2)}) collective-permute-start(bf16[176,2048]{1,0:T(8,128)(2,1)} %collective-permute-done.8.refs_7_), channel_id=1, source_target_pairs={{1,0},{0,1},{3,2},{2,3},{5,4},{4,5},{7,6},{6,7},{9,8},{8,9},{11,10... | collective-permute-start | bytes 2162696 | tf_op jit(solution)/shard_map/ppermute | solution.py:27
  133.7 3.0 %collective-permute-start.2 = (bf16[64,2176]{1,0:T(8,128)(2,1)S(1)}, bf16[64,2176]{1,0:T(8,128)(2,1)S(1)}, u32[]{:S(2)}, u32[]{:S(2)}) collective-permute-start(bf16[64,2176]{1,0:T(8,128)(2,1)S(1)} %all_gather.3.refs_0_), channel_id=1, source_target_pairs={{248,0},{9,1},{0,8},{17,9},{8,16},{25,17},{16,24},{33,25},{24,32},... | collective-permute-start | bytes 835592 | tf_op jit(solution)/shard_map/ppermute | solution.py:22
  136.7 7.7 %collective-permute-done.2.refs_3_ = bf16[64,2176]{1,0:T(8,128)(2,1)S(1)} collective-permute-done((bf16[64,2176]{1,0:T(8,128)(2,1)S(1)}, bf16[64,2176]{1,0:T(8,128)(2,1)S(1)}, u32[]{:S(2)}, u32[]{:S(2)}) %collective-permute-start.2) | collective-permute-done | bytes 278560 | tf_op jit(solution)/shard_map/ppermute | solution.py:22
  145.3 5.1 %collective-permute-start.3 = (bf16[64,2048]{1,0:T(8,128)(2,1)S(1)}, bf16[64,2048]{1,0:T(8,128)(2,1)S(1)}, u32[]{:S(2)}, u32[]{:S(2)}) collective-permute-start(bf16[64,2048]{1,0:T(8,128)(2,1)S(1)} %get-tuple-element.13.own_ref), channel_id=1, source_target_pairs={{6,0},{4,2},{2,4},{0,6},{7,1},{5,3},{3,5},{1,7},{14,8},{12,10},{10... | collective-permute-start | bytes 786440 | tf_op jit(solution)/shard_map/ppermute | solution.py:58
  150.4 4.4 %collective-permute-done.3.other_ref = bf16[64,2048]{1,0:T(8,128)(2,1)S(1)} collective-permute-done((bf16[64,2048]{1,0:T(8,128)(2,1)S(1)}, bf16[64,2048]{1,0:T(8,128)(2,1)S(1)}, u32[]{:S(2)}, u32[]{:S(2)}) %collective-permute-start.3) | collective-permute-done | bytes 262176 | tf_op jit(solution)/shard_map/ppermute | solution.py:58
  156.2 4.9 %shard_map.93 = (f32[64,2048]{1,0:T(8,128)S(1)}, bf16[64,2048]{1,0:T(8,128)(2,1)S(1)}) custom-call(bf16[64,2048]{1,0:T(8,128)(2,1)S(1)} %get-tuple-element.13.own_ref, bf16[64,2048]{1,0:T(8,128)(2,1)S(1)} %collective-permute-done.3.other_ref, bf16[2,176,2048]{2,1,0:T(8,128)(2,1)S(1)} %bitcast.13, bf16[2,176,2048]{2,1,0:T(8,128)(2,1)} %collective-permute-done.4.refs_1_, ...), custom_call_target="tpu_custom_call" | custom-call | flops 1107296256 | bytes 8650752 | tf_op jit(solution)/shard_map/pallas_call | solution.py:104
  161.1 5.1 %collective-permute-start.10 = (bf16[64,2048]{1,0:T(8,128)(2,1)S(1)}, bf16[64,2048]{1,0:T(8,128)(2,1)S(1)}, u32[]{:S(2)}, u32[]{:S(2)}) collective-permute-start(bf16[64,2048]{1,0:T(8,128)(2,1)S(1)} %get-tuple-element.15), channel_id=1, source_target_pairs={{6,0},{4,2},{2,4},{0,6},{7,1},{5,3},{3,5},{1,7},{14,8},{12,10},{10... | collective-permute-start | bytes 786440 | tf_op jit(solution)/shard_map/ppermute | solution.py:58
  166.2 2.3 shard_map.94.shared_ref
  168.5 2.0 collective-permute-done.10.got_ref
  171.0 2.0 collective-permute-start.11
  172.9 2.0 collective-permute-start.12
  174.9 5.2 %collective-permute-start.13 = (bf16[64,2048]{1,0:T(8,128)(2,1)S(1)}, bf16[64,2048]{1,0:T(8,128)(2,1)S(1)}, u32[]{:S(2)}, u32[]{:S(2)}) collective-permute-start(bf16[64,2048]{1,0:T(8,128)(2,1)S(1)} %get-tuple-element.20), channel_id=1, source_target_pairs={{8,0},{249,1},{16,8},{1,9},{24,16},{9,17},{32,24},{17,25},{40,32},... | collective-permute-start | bytes 786440 | tf_op jit(solution)/shard_map/ppermute | solution.py:22
  181.3 8.2 %collective-permute-done.12 = bf16[64,2048]{1,0:T(8,128)(2,1)S(1)} collective-permute-done((bf16[64,2048]{1,0:T(8,128)(2,1)S(1)}, bf16[64,2048]{1,0:T(8,128)(2,1)S(1)}, u32[]{:S(2)}, u32[]{:S(2)}) %collective-permute-start.12) | collective-permute-done | bytes 262176 | tf_op jit(solution)/shard_map/ppermute | solution.py:22
  189.6 51.4 %all_to_all.5 = bf16[8,8,2048]{2,1,0:T(8,128)(2,1)S(1)} all-to-all(bf16[8,8,2048]{2,1,0:T(8,128)(2,1)S(1)} %fusion), channel_id=1, replica_groups={{0,32,64,96,128,160,192,224},{8,40,72,104,136,168,200,232},{16,48,80,11..., dimensions={0} | all-to-all | bytes 524288 | tf_op jit(solution)/shard_map/all_to_all | solution.py:45
  (24 shorter events, 7.1 us)
Async XLA Ops:
  0.0 36.7 %collective-permute-start.5 = (bf16[2,176,2048]{2,1,0:T(8,128)(2,1)}, bf16[2,176,2048]{2,1,0:T(8,128)(2,1)}, u32[]{:S(2)}, u32[]{:S(2)}) collective-permute-start(bf16[2,176,2048]{2,1,0:T(8,128)(2,1)} %bitcast.11), channel_id=1, source_target_pairs={{2,0},{0,2},{6,4},{4,6},{3,1},{1,3},{7,5},{5,7},{10,8},{8,10},{14,... | collective-permute-start | bytes 4325384 | tf_op jit(solution)/shard_map/ppermute | solution.py:58
  3.6 126.8 %collective-permute-start.8 = (bf16[176,2048]{1,0:T(8,128)(2,1)}, bf16[176,2048]{1,0:T(8,128)(2,1)}, u32[]{:S(2)}, u32[]{:S(2)}) collective-permute-start(bf16[176,2048]{1,0:T(8,128)(2,1)} %bitcast.15), channel_id=1, source_target_pairs={{2,0},{0,2},{6,4},{4,6},{3,1},{1,3},{7,5},{5,7},{10,8},{8,10},{14,... | collective-permute-start | bytes 2162696 | tf_op jit(solution)/shard_map/ppermute | solution.py:58
  5.9 148.9 %collective-permute-start.4 = (bf16[2,176,2048]{2,1,0:T(8,128)(2,1)}, bf16[2,176,2048]{2,1,0:T(8,128)(2,1)}, u32[]{:S(2)}, u32[]{:S(2)}) collective-permute-start(bf16[2,176,2048]{2,1,0:T(8,128)(2,1)} %bitcast.12), channel_id=1, source_target_pairs={{1,0},{0,1},{3,2},{2,3},{5,4},{4,5},{7,6},{6,7},{9,8},{8,9},{11,10... | collective-permute-start | bytes 4325384 | tf_op jit(solution)/shard_map/ppermute | solution.py:27
  36.7 118.1 %collective-permute-start.6 = (bf16[2,176,2048]{2,1,0:T(8,128)(2,1)}, bf16[2,176,2048]{2,1,0:T(8,128)(2,1)}, u32[]{:S(2)}, u32[]{:S(2)}) collective-permute-start(bf16[2,176,2048]{2,1,0:T(8,128)(2,1)} %collective-permute-done.5.refs_3_), channel_id=1, source_target_pairs={{1,0},{0,1},{3,2},{2,3},{5,4},{4,5},{7,6},{6,7},{9,8},{8,9},{11,10... | collective-permute-start | bytes 4325384 | tf_op jit(solution)/shard_map/ppermute | solution.py:27
  40.2 114.6 %copy-start.2 = (bf16[1,176,2048]{2,1,0:T(8,128)(2,1)S(1)}, bf16[1,176,2048]{2,1,0:T(8,128)(2,1)}, u32[]{:S(2)}) copy-start(bf16[1,176,2048]{2,1,0:T(8,128)(2,1)} %param.17) | copy-start | bytes 2162692
  113.8 14.6 %collective-permute-start = (bf16[64,2176]{1,0:T(8,128)(2,1)S(1)}, bf16[64,2176]{1,0:T(8,128)(2,1)S(1)}, u32[]{:S(2)}, u32[]{:S(2)}) collective-permute-start(bf16[64,2176]{1,0:T(8,128)(2,1)S(1)} %all_gather.3.refs_0_), channel_id=1, source_target_pairs={{8,0},{249,1},{16,8},{1,9},{24,16},{9,17},{32,24},{17,25},{40,32},... | collective-permute-start | bytes 835592 | tf_op jit(solution)/shard_map/ppermute | solution.py:22
  124.2 9.5 %collective-permute-start.1 = (bf16[64,2176]{1,0:T(8,128)(2,1)S(1)}, bf16[64,2176]{1,0:T(8,128)(2,1)S(1)}, u32[]{:S(2)}, u32[]{:S(2)}) collective-permute-start(bf16[64,2176]{1,0:T(8,128)(2,1)S(1)} %all_gather.3.refs_0_), channel_id=1, source_target_pairs={{16,0},{241,1},{24,8},{249,9},{32,16},{1,17},{40,24},{9,25},{48,32... | collective-permute-start | bytes 835592 | tf_op jit(solution)/shard_map/ppermute | solution.py:22
  128.4 26.4 %collective-permute-start.7 = (bf16[176,2048]{1,0:T(8,128)(2,1)}, bf16[176,2048]{1,0:T(8,128)(2,1)S(1)}, u32[]{:S(2)}, u32[]{:S(2)}) collective-permute-start(bf16[176,2048]{1,0:T(8,128)(2,1)} %bitcast.16), channel_id=1, source_target_pairs={{1,0},{0,1},{3,2},{2,3},{5,4},{4,5},{7,6},{6,7},{9,8},{8,9},{11,10... | collective-permute-start | bytes 2162696 | tf_op jit(solution)/shard_map/ppermute | solution.py:27
  130.4 24.4 %collective-permute-start.9 = (bf16[176,2048]{1,0:T(8,128)(2,1)}, bf16[176,2048]{1,0:T(8,128)(2,1)S(1)}, u32[]{:S(2)}, u32[]{:S(2)}) collective-permute-start(bf16[176,2048]{1,0:T(8,128)(2,1)} %collective-permute-done.8.refs_7_), channel_id=1, source_target_pairs={{1,0},{0,1},{3,2},{2,3},{5,4},{4,5},{7,6},{6,7},{9,8},{8,9},{11,10... | collective-permute-start | bytes 2162696 | tf_op jit(solution)/shard_map/ppermute | solution.py:27
  133.7 10.7 %collective-permute-start.2 = (bf16[64,2176]{1,0:T(8,128)(2,1)S(1)}, bf16[64,2176]{1,0:T(8,128)(2,1)S(1)}, u32[]{:S(2)}, u32[]{:S(2)}) collective-permute-start(bf16[64,2176]{1,0:T(8,128)(2,1)S(1)} %all_gather.3.refs_0_), channel_id=1, source_target_pairs={{248,0},{9,1},{0,8},{17,9},{8,16},{25,17},{16,24},{33,25},{24,32},... | collective-permute-start | bytes 835592 | tf_op jit(solution)/shard_map/ppermute | solution.py:22
  144.4 21.8 %copy-start.4 = (bf16[2048]{0:T(1024)(128)(2,1)S(1)}, bf16[2048]{0:T(1024)(128)(2,1)}, u32[]{:S(2)}) copy-start(bf16[2048]{0:T(1024)(128)(2,1)} %param.13) | copy-start | bytes 12292
  145.3 9.5 %collective-permute-start.3 = (bf16[64,2048]{1,0:T(8,128)(2,1)S(1)}, bf16[64,2048]{1,0:T(8,128)(2,1)S(1)}, u32[]{:S(2)}, u32[]{:S(2)}) collective-permute-start(bf16[64,2048]{1,0:T(8,128)(2,1)S(1)} %get-tuple-element.13.own_ref), channel_id=1, source_target_pairs={{6,0},{4,2},{2,4},{0,6},{7,1},{5,3},{3,5},{1,7},{14,8},{12,10},{10... | collective-permute-start | bytes 786440 | tf_op jit(solution)/shard_map/ppermute | solution.py:58
  154.8 1.4 copy-start
  156.2 10.0 %copy-start.1 = (bf16[2,2048,176]{1,2,0:T(8,128)(2,1)S(1)}, bf16[2,2048,176]{1,2,0:T(8,128)(2,1)}, u32[]{:S(2)}) copy-start(bf16[2,2048,176]{1,2,0:T(8,128)(2,1)} %param.14) | copy-start | bytes 4325380
  156.2 10.0 %copy-start.3 = (bf16[176,2048]{1,0:T(8,128)(2,1)S(1)}, bf16[176,2048]{1,0:T(8,128)(2,1)}, u32[]{:S(2)}) copy-start(bf16[176,2048]{1,0:T(8,128)(2,1)} %refs_6_.1) | copy-start | bytes 2162692
  161.1 9.5 %collective-permute-start.10 = (bf16[64,2048]{1,0:T(8,128)(2,1)S(1)}, bf16[64,2048]{1,0:T(8,128)(2,1)S(1)}, u32[]{:S(2)}, u32[]{:S(2)}) collective-permute-start(bf16[64,2048]{1,0:T(8,128)(2,1)S(1)} %get-tuple-element.15), channel_id=1, source_target_pairs={{6,0},{4,2},{2,4},{0,6},{7,1},{5,3},{3,5},{1,7},{14,8},{12,10},{10... | collective-permute-start | bytes 786440 | tf_op jit(solution)/shard_map/ppermute | solution.py:58
  171.0 10.3 %collective-permute-start.11 = (bf16[64,2048]{1,0:T(8,128)(2,1)S(1)}, bf16[64,2048]{1,0:T(8,128)(2,1)S(1)}, u32[]{:S(2)}, u32[]{:S(2)}) collective-permute-start(bf16[64,2048]{1,0:T(8,128)(2,1)S(1)} %get-tuple-element.18), channel_id=1, source_target_pairs={{248,0},{9,1},{0,8},{17,9},{8,16},{25,17},{16,24},{33,25},{24,32},... | collective-permute-start | bytes 786440 | tf_op jit(solution)/shard_map/ppermute | solution.py:22
  172.9 16.6 %collective-permute-start.12 = (bf16[64,2048]{1,0:T(8,128)(2,1)S(1)}, bf16[64,2048]{1,0:T(8,128)(2,1)S(1)}, u32[]{:S(2)}, u32[]{:S(2)}) collective-permute-start(bf16[64,2048]{1,0:T(8,128)(2,1)S(1)} %get-tuple-element.19), channel_id=1, source_target_pairs={{240,0},{17,1},{248,8},{25,9},{0,16},{33,17},{8,24},{41,25},{16,32... | collective-permute-start | bytes 786440 | tf_op jit(solution)/shard_map/ppermute | solution.py:22
  174.9 14.6 %collective-permute-start.13 = (bf16[64,2048]{1,0:T(8,128)(2,1)S(1)}, bf16[64,2048]{1,0:T(8,128)(2,1)S(1)}, u32[]{:S(2)}, u32[]{:S(2)}) collective-permute-start(bf16[64,2048]{1,0:T(8,128)(2,1)S(1)} %get-tuple-element.20), channel_id=1, source_target_pairs={{8,0},{249,1},{16,8},{1,9},{24,16},{9,17},{32,24},{17,25},{40,32},... | collective-permute-start | bytes 786440 | tf_op jit(solution)/shard_map/ppermute | solution.py:22
